TPU v7x, 32 devices: a whole 2x2x4 slice. The times are simulated.
32 devices in a mesh: seq: 8 (over z, y), tp: 4 (over x, core).
Axes of the slice: x: 2, y: 2, z: 4, core: 2. Of those that a mesh axis runs over, the one named last changes fastest.
Arguments:
- tokens: bfloat16 [8192, 2048], P('seq', 'tp'), may hold values from -8 to 8
- col_order: int32 [8192], P('seq'), may hold values from 0 to 8191, as said below
- in_gain: float32 [2, 2048], replicated, may hold values from 0.5 to 1.5
- w_in: bfloat16 [2, 2048, 2, 2048], P(None, None, None, 'tp'), may hold values from -0.125 to 0.125
- w_bc: bfloat16 [2, 2048, 256], replicated, may hold values from -0.0625 to 0.0625
- w_dt: bfloat16 [2, 2048, 32], P(None, None, 'tp'), may hold values from -2 to 2
- conv_x: float32 [2, 4, 2048], P(None, None, 'tp'), may hold values from -3 to 3
- conv_bc: float32 [2, 4, 256], replicated, may hold values from -3 to 3
- dt_bias: float32 [2, 32], P(None, 'tp'), may hold values from -1 to 0.5
- a_log: float32 [2, 32], P(None, 'tp'), may hold values from -16 to -2, as said below
- d_skip: float32 [2, 32], P(None, 'tp'), may hold values from 0.5 to 2
- out_gain: float32 [2, 2048], P(None, 'tp'), may hold values from 0.5 to 1.5
- w_out: bfloat16 [2, 2048, 2048], P(None, 'tp'), may hold values from -0.125 to 0.125
Outputs:
- mixed_out: bfloat16 [8192, 2048], P('seq', 'tp')
Inputs may be any that keep to these rules, and one draw needn't show every extreme that they name: `col_order`: A permutation of the 8192 positions of a frame of 16 rows and 512 columns stored row by row: the column order visits the columns one after another in a drawn order, each from top to bottom or from bottom to top as drawn. So every aligned block of 1024 positions takes exactly 128 row-order positions from each aligned block of 1024 row-order positions. Each head's decay rate exp(a_log) is either between about one in fifty and one in seventeen a step or between 0.3 / 8192 and 2 / 8192 a step.
All inputs are finite; a program needn't handle non-finite values.
Results may differ from a plain program's by a relative error of at most 0.024.
Values may be sent and summed in bfloat16 or wider, within the bound.
A program may use at most 128 MiB of HBM per device.

v0:
```python
import jax
import jax.numpy as jnp
from jax import lax
from jax.sharding import PartitionSpec as P

HEAD_DIM = 64
STATE = 128
STRETCH = 128


highest = lax.Precision.HIGHEST
epsilon = 1e-05


def passed_along(x, axis, by):
    devices = lax.axis_size(axis)
    pairs = [(i, i + by) for i in range(devices) if 0 <= i + by < devices]
    return lax.ppermute(x, axis, pairs)


def causal_mix(current, rim, taps):
    length = current.shape[0]
    extended = jnp.concatenate([rim, current], axis=0).astype(jnp.float32)
    mixed = jnp.zeros(current.shape, jnp.float32)
    for offset in range(taps.shape[0]):
        mixed = mixed + taps[offset] * extended[offset : offset + length]
    return mixed


def advance(state, pieces):
    factor, fresh = pieces
    return (factor[:, None, None] * state + fresh, state)


def incoming_state(local_end, device_log):
    count = lax.axis_size("seq")
    own_index = lax.axis_index("seq")
    gathered = lax.all_gather(device_log, "seq", axis=0, tiled=True).reshape(
        count, device_log.shape[0]
    )
    before = jnp.cumsum(gathered, axis=0) - gathered
    earlier = (jnp.arange(count) < own_index)[:, None]
    own_prefix = jnp.sum(jnp.where(earlier, gathered, 0.0), axis=0)
    spans = jnp.where(earlier, own_prefix[None, :] - before - gathered, -jnp.inf)
    factors = jnp.exp(spans)
    return jnp.zeros(local_end.shape, jnp.float32) + jnp.einsum(
        "mh,mhpn->hpn",
        factors,
        lax.all_gather(local_end[None].astype(jnp.bfloat16), "seq", axis=0, tiled=True).astype(
            jnp.float32
        ),
        precision=highest,
    )


def mixer(full, which, params):
    in_gain, w_in, w_bc, w_dt, conv_x, conv_bc, dt_bias, a_log, d_skip, out_gain, w_out = params
    row_count, model_width = full.shape
    inner = w_in.shape[3]
    head_count = inner // HEAD_DIM
    lag = conv_x.shape[1] - 1
    widen = full.astype(jnp.float32)
    scale = lax.rsqrt(jnp.mean(widen * widen, axis=-1, keepdims=True) + epsilon)
    normed = (widen * scale * in_gain[which]).astype(jnp.bfloat16)
    projected = jnp.dot(
        normed, w_in[which].reshape(model_width, 2 * inner), preferred_element_type=jnp.float32
    )
    pre_x = projected[:, :inner].astype(jnp.bfloat16)
    gate_z = projected[:, inner:].astype(jnp.bfloat16)
    pre_bc = jnp.dot(normed, w_bc[which], preferred_element_type=jnp.float32).astype(jnp.bfloat16)
    dt_raw = jnp.dot(normed, w_dt[which], preferred_element_type=jnp.float32)
    rim_x, rim_bc = passed_along((pre_x[row_count - lag :], pre_bc[row_count - lag :]), "seq", 1)
    conv_out = jax.nn.silu(causal_mix(pre_x, rim_x, conv_x[which]))
    bc_out = jax.nn.silu(causal_mix(pre_bc, rim_bc, conv_bc[which]))
    step_size = jax.nn.softplus(dt_raw + dt_bias[which])
    decay_log = -step_size * jnp.exp(a_log[which])
    heads_in = conv_out.reshape(row_count, head_count, HEAD_DIM)
    feed = heads_in * step_size[:, :, None]
    blocks = row_count // STRETCH
    log_blocks = decay_log.reshape(blocks, STRETCH, head_count)
    b_blocks = bc_out[:, :STATE].reshape(blocks, STRETCH, STATE)
    c_blocks = bc_out[:, STATE:].reshape(blocks, STRETCH, STATE)
    feed_blocks = feed.reshape(blocks, STRETCH, head_count, HEAD_DIM)
    cumul = jnp.cumsum(log_blocks, axis=1)
    cumul_t = jnp.transpose(cumul, (0, 2, 1))
    lower = jnp.arange(STRETCH)[:, None] >= jnp.arange(STRETCH)[None, :]
    spread = jnp.where(lower[None, None], cumul_t[..., :, None] - cumul_t[..., None, :], -jnp.inf)
    intersection = jnp.einsum("cqn,ckn->cqk", c_blocks, b_blocks, precision=highest)
    inside = jnp.einsum(
        "chqk,ckhp->cqhp", intersection[:, None] * jnp.exp(spread), feed_blocks, precision=highest
    )
    to_end = jnp.exp(cumul_t[..., -1:] - cumul_t)
    fresh = jnp.einsum("chk,ckn,ckhp->chpn", to_end, b_blocks, feed_blocks, precision=highest)
    block_decay = jnp.exp(cumul_t[..., -1])
    start_state = jnp.zeros((head_count, HEAD_DIM, STATE), jnp.float32)
    local_end, entering = lax.scan(advance, start_state, (block_decay, fresh))
    carried = (
        jnp.einsum("cqn,chpn->cqhp", c_blocks, entering, precision=highest)
        * jnp.exp(cumul)[..., None]
    )
    block_sums = cumul[:, -1, :]
    prior = jnp.cumsum(block_sums, axis=0) - block_sums
    device_cumul = cumul + prior[:, None, :]
    device_log = jnp.sum(block_sums, axis=0)
    arriving = incoming_state(local_end, device_log)
    correction = (
        jnp.einsum("cqn,hpn->cqhp", c_blocks, arriving, precision=highest)
        * jnp.exp(device_cumul)[..., None]
    )
    ssd = (inside + carried + correction).reshape(row_count, head_count, HEAD_DIM) + d_skip[which][
        None, :, None
    ] * heads_in
    gated = ssd * jax.nn.silu(gate_z.astype(jnp.float32).reshape(row_count, head_count, HEAD_DIM))
    norm_scale = lax.rsqrt(jnp.mean(gated * gated, axis=-1, keepdims=True) + epsilon)
    mixed_heads = (
        (gated * norm_scale * out_gain[which].reshape(head_count, HEAD_DIM))
        .reshape(row_count, inner)
        .astype(jnp.bfloat16)
    )
    return jnp.dot(mixed_heads, w_out[which], preferred_element_type=jnp.float32)


def spread_features(piece):
    return lax.all_gather(piece, "tp", axis=1, tiled=True)


def collect_heads(partial_sum):
    return lax.psum_scatter(
        partial_sum.astype(jnp.bfloat16), "tp", scatter_dimension=1, tiled=True
    ).astype(jnp.float32)


def reorder_rows(stream, col_order):
    count = lax.axis_size("seq")
    row_count = stream.shape[0]
    block_rows = row_count // count
    source = col_order // row_count
    local_index = col_order % row_count
    grouping = jnp.argsort(source, stable=True)
    wanted = local_index[grouping].reshape(count, block_rows)
    asked = lax.all_to_all(wanted, "seq", split_axis=0, concat_axis=0, tiled=True)
    payload = stream[asked.reshape(-1)].reshape(count, block_rows, stream.shape[1])
    arrived = lax.all_to_all(payload, "seq", split_axis=0, concat_axis=0, tiled=True).reshape(
        row_count, stream.shape[1]
    )
    placement = jnp.argsort(grouping)
    return arrived[placement]


def body(
    tokens,
    col_order,
    in_gain,
    w_in,
    w_bc,
    w_dt,
    conv_x,
    conv_bc,
    dt_bias,
    a_log,
    d_skip,
    out_gain,
    w_out,
):
    params = (in_gain, w_in, w_bc, w_dt, conv_x, conv_bc, dt_bias, a_log, d_skip, out_gain, w_out)
    first_full = spread_features(tokens)
    first_part = mixer(first_full, 0, params)
    row_result = (tokens.astype(jnp.float32) + collect_heads(first_part)).astype(jnp.bfloat16)
    own_rows = reorder_rows(row_result, col_order)
    second_full = spread_features(own_rows)
    second_part = mixer(second_full, 1, params)
    return (own_rows.astype(jnp.float32) + collect_heads(second_part)).astype(jnp.bfloat16)


def solution(mesh):
    placed = (
        P("seq", "tp"),
        P("seq"),
        P(),
        P(None, None, None, "tp"),
        P(),
        P(None, None, "tp"),
        P(None, None, "tp"),
        P(),
        P(None, "tp"),
        P(None, "tp"),
        P(None, "tp"),
        P(None, "tp"),
        P(None, "tp", None),
    )
    return jax.shard_map(
        body, mesh=mesh, in_specs=placed, out_specs=P("seq", "tp"), check_vma=False
    )
```

profile of v0, /device:TPU:0, one launch (start us, length us, event | category | flops | bytes accessed | tf_op | source)
XLA Modules:
  0.0 541.5 jit_solution(10264184427575048741)
XLA Ops:
  7.3 7.9 %fusion.98 = (bf16[1,2048,2,512]{3,2,1,0:T(2,128)(2,1)}, bf16[1,2048,2,512]{3,2,1,0:T(2,128)(2,1)S(1)}) fusion(bf16[2,2048,2,512]{3,2,1,0:T(2,128)(2,1)} %param.20), kind=kLoop, calls=%fused_computation.187 | loop fusion | bytes 16777216 | tf_op jit(solution)/shard_map/slice | solution.py:66
  22.1 24.0 %all-gather.8.cloned.1.call-done = bf16[1024,2048]{1,0:T(8,128)(2,1)} async-done(((bf16[1024,512]{1,0:T(8,128)(2,1)}), bf16[1024,2048]{1,0:T(8,128)(2,1)}) %all-gather.8.cloned.1.call-update) | async-done | bytes 4194320 | tf_op jit(solution)/shard_map/all_gather | solution.py:124
  49.6 7.2 %convolution_convert_fusion.3 = bf16[1024,1024]{1,0:T(8,128)(2,1)S(1)} fusion(bf16[2048,1024]{1,0:T(8,128)(2,1)} %bitcast.224, bf16[1024,2048]{1,0:T(8,128)(2,1)S(1)} %copy-done.14, f32[2048]{0:T(1024)S(1)} %bitcast.245, f32[1024]{0:T(1024)S(1)} %add_rsqrt_fusion.1), kind=kOutput, calls=%fused_computation.88 | convolution fusion | flops 4304404480 | bytes 10498048 | tf_op jit(solution)/shard_map/dot_general | solution.py:65
  60.7 23.3 %fusion.107 = f32[8,128,8]{2,0,1:T(8,128)S(1)} fusion(f32[8,128,8]{2,0,1:T(8,128)S(1)} %copy.72), kind=kOutput, calls=%fused_computation.196 | output fusion | flops 1040384 | bytes 65536 | tf_op jit(solution)/shard_map/jit(cumsum)/reduce_window_sum | solution.py:84
  117.0 19.6 %while.26 = (s32[]{:T(128)}, f32[8,64,128]{2,1,0:T(8,128)S(1)}, f32[8,8,64,128]{3,2,1,0:T(8,128)}, f32[8,8]{1,0:T(8,128)}, f32[8,8,64,128]{3,2,1,0:T(8,128)}, /*index=5*/s32[]{:T(128)}, s32[]{:T(128)}) while((s32[]{:T(128)}, f32[8,64,128]{2,1,0:T(8,128)S(1)}, f32[8,8,64,128]{3,2,1,0:T(8,128)}, f32[8,8]{1,0:T(8,128)}, ...), condition=%wide.region_3.4_spmd.clone, body=%wide.region_2.3_spmd.clone.sunk | while | flops 262147 | bytes 1311424 | solution.py:96
  139.3 20.8 %all-reduce = f32[64]{0:T(128)S(1)} all-reduce(f32[64]{0:T(128)S(1)} %dynamic-update-slice), channel_id=1, replica_groups=mesh['seq'=8,'tp'=4] {'seq'}, use_global_device_ids=true, to_apply=%add | all-reduce | flops 64 | bytes 512
  175.2 9.7 %fusion.13 = f32[8,8,64,128]{3,2,1,0:T(8,128)} fusion(f32[8,128,8,64]{1,0,3,2:T(8,128)S(1)} %copy-done.18, f32[8,8,128]{2,1,0:T(8,128)S(1)} %copy.73, f32[8,128,128]{2,1,0:T(8,128)S(1)} %fusion.109, pred[128,128]{1,0:T(8,128)(4,1)S(1)} %iota_compare_fusion), kind=kOutput, calls=%fused_computation.26 | convolution fusion | flops 808452096 | bytes 4767744 | tf_op jit(solution)/shard_map/chqk,ckhp->cqhp/dot_general | solution.py:89
  187.3 7.2 %fusion.38 = (f32[8,128,8]{1,2,0:T(8,128)S(1)}, f32[8,128,8,64]{1,3,2,0:T(8,128)}) fusion(f32[8,128,8,64]{1,0,3,2:T(8,128)S(1)} %bitcast.207, f32[8,128,8,64]{1,3,2,0:T(8,128)} %copy.85, f32[8]{0:T(128)S(1)} %copy-done.33, f32[8,128,8]{1,2,0:T(8,128)S(1)} %copy.79, f32[8,128,128,1]{2,1,3,0:T(8,128)S(1)} %bitcast.216, f32[8,64,128,1]{2,1,0,3:T(8,128)S(1)} %bitcast.228, ...), kind=kOutput, calls=%fused_computation.65 | convolution fusion | flops 812113920 | bytes 11370528 | tf_op jit(solution)/shard_map/cqn,hpn->cqhp/dot_general | solution.py:107
  205.2 8.5 %convolution_convert_fusion.1 = bf16[1024,2048]{1,0:T(8,128)(2,1)} fusion(bf16[2,512,2048]{2,1,0:T(8,128)(2,1)} %param.29, f32[1024,512]{1,0:T(8,128)} %copy.86, f32[1024,512]{1,0:T(8,128)} %reshape.312, f32[1024,512]{1,0:T(8,128)} %divide_multiply_fusion.1, f32[512]{0:T(512)S(1)} %bitcast.257, f32[512]{0:T(512)S(1)} %mul.493, bf16[1024,1024]{1,0:T(8,128)(2,1)} %copy-done.16), kind=kOutput, calls=%fused_computation.32 | convolution fusion | flops 2155347968 | bytes 13635584 | tf_op jit(solution)/shard_map/dot_general | solution.py:120
  223.3 8.9 %all_to_all.14 = s32[8,1,128]{2,1,0:T(1,128)S(1)} all-to-all(s32[8,1,128]{2,1,0:T(1,128)S(1)} %bitcast.233), channel_id=1, replica_groups=mesh['seq'=8,'tp'=4] {'seq'}, dimensions={0} | all-to-all | bytes 8192 | tf_op jit(solution)/shard_map/all_to_all | solution.py:141
  232.2 22.5 %reduce-scatter.3.cloned.1.call-done = bf16[1024,512]{1,0:T(8,128)(2,1)} async-done(((bf16[1024,2048]{1,0:T(8,128)(2,1)}), bf16[1024,512]{1,0:T(8,128)(2,1)}) %reduce-scatter.3.cloned.1.call-update) | async-done | bytes 1048592 | tf_op jit(solution)/shard_map/reduce_scatter | solution.py:128
  256.2 5.1 gather_fusion.1
  261.3 5.5 %all-to-all-start.1 = ((bf16[8,128,512]{2,1,0:T(8,128)(2,1)}), bf16[8,128,512]{2,1,0:T(8,128)(2,1)S(1)}, u32[]{:S(2)}, u32[]{:S(2)}) async-start(bf16[8,128,512]{2,1,0:T(8,128)(2,1)} %bitcast.42), calls=%async_computation.2 | async-start | bytes 2097152 | tf_op jit(solution)/shard_map/all_to_all | solution.py:143
  271.2 21.2 %all-to-all-done.1 = bf16[8,128,512]{2,1,0:T(8,128)(2,1)S(1)} async-done(((bf16[8,128,512]{2,1,0:T(8,128)(2,1)}), bf16[8,128,512]{2,1,0:T(8,128)(2,1)S(1)}, u32[]{:S(2)}, u32[]{:S(2)}) %all-to-all-start.1) | async-done | bytes 1048608 | tf_op jit(solution)/shard_map/all_to_all | solution.py:143
  297.6 5.5 %copy.124 = bf16[256,8,2,512]{3,1,2,0:T(8,128)(2,1)} copy(bf16[256,8,2,512]{3,2,1,0:T(2,128)(2,1)} %bitcast.198) | data formatting | bytes 8388608
  303.1 27.1 %all-gather.12.cloned.1.call-done = bf16[1024,2048]{1,0:T(8,128)(2,1)} async-done(((bf16[1024,512]{1,0:T(8,128)(2,1)}), bf16[1024,2048]{1,0:T(8,128)(2,1)}) %all-gather.12.cloned.1.call-update) | async-done | bytes 4194320 | tf_op jit(solution)/shard_map/all_gather | solution.py:124
  341.6 23.3 %fusion.108 = f32[8,128,8]{2,0,1:T(8,128)S(1)} fusion(f32[8,128,8]{2,0,1:T(8,128)S(1)} %copy.89), kind=kOutput, calls=%fused_computation.197 | output fusion | flops 1040384 | bytes 65536 | tf_op jit(solution)/shard_map/jit(cumsum)/reduce_window_sum | solution.py:84
  365.0 8.0 %convolution_convert_fusion.2 = bf16[1024,1024]{1,0:T(8,128)(2,1)S(1)} fusion(bf16[2048,1024]{1,0:T(8,128)(2,1)} %bitcast.225, bf16[1024,2048]{1,0:T(8,128)(2,1)} %all-gather.12.cloned.1.call-done, f32[2048]{0:T(1024)S(1)} %bitcast.244, f32[1024]{0:T(1024)S(1)} %add_rsqrt_fusion), kind=kOutput, calls=%fused_computation.87 | convolution fusion | flops 4304404480 | bytes 10498048 | tf_op jit(solution)/shard_map/dot_general | solution.py:65
  397.7 19.8 %while.27 = (s32[]{:T(128)}, f32[8,64,128]{2,1,0:T(8,128)S(1)}, f32[8,8,64,128]{3,2,1,0:T(8,128)}, f32[8,8]{1,0:T(8,128)}, f32[8,8,64,128]{3,2,1,0:T(8,128)}, /*index=5*/s32[]{:T(128)}, s32[]{:T(128)}) while((s32[]{:T(128)}, f32[8,64,128]{2,1,0:T(8,128)S(1)}, f32[8,8,64,128]{3,2,1,0:T(8,128)}, f32[8,8]{1,0:T(8,128)}, ...), condition=%wide.region_15.16_spmd.clone, body=%wide.region_14.15_spmd.clone.sunk | while | flops 262147 | bytes 1311424 | solution.py:96
  418.9 18.7 %all-reduce.1 = f32[64]{0:T(128)S(1)} all-reduce(f32[64]{0:T(128)S(1)} %dynamic-update-slice.1), channel_id=1, replica_groups=mesh['seq'=8,'tp'=4] {'seq'}, use_global_device_ids=true, to_apply=%add.1 | all-reduce | flops 64 | bytes 512
  452.5 9.6 %fusion.8 = f32[8,8,64,128]{3,2,1,0:T(8,128)} fusion(f32[8,128,8,64]{1,0,3,2:T(8,128)S(1)} %copy-done.19, f32[8,8,128]{2,1,0:T(8,128)S(1)} %copy.90, f32[8,128,128]{2,1,0:T(8,128)S(1)} %fusion.111, pred[128,128]{1,0:T(8,128)(4,1)S(1)} %iota_compare_fusion), kind=kOutput, calls=%fused_computation.21 | convolution fusion | flops 808452096 | bytes 4767744 | tf_op jit(solution)/shard_map/chqk,ckhp->cqhp/dot_general | solution.py:89
  464.6 7.2 %fusion.31 = (f32[8,128,8]{1,2,0:T(8,128)S(1)}, f32[8,128,8,64]{1,3,2,0:T(8,128)}) fusion(f32[8,128,8,64]{1,0,3,2:T(8,128)S(1)} %bitcast.209, f32[8,128,8,64]{1,3,2,0:T(8,128)} %copy.102, f32[8]{0:T(128)S(1)} %copy-done.32, f32[8,128,8]{1,2,0:T(8,128)S(1)} %copy.96, f32[8,128,128,1]{2,1,3,0:T(8,128)S(1)} %bitcast.219, f32[8,64,128,1]{2,1,0,3:T(8,128)S(1)} %bitcast.229, ...), kind=kOutput, calls=%fused_computation.57 | convolution fusion | flops 812113920 | bytes 11370528 | tf_op jit(solution)/shard_map/cqn,hpn->cqhp/dot_general | solution.py:107
  482.5 8.4 %convolution_convert_fusion = bf16[1024,2048]{1,0:T(8,128)(2,1)} fusion(bf16[2,512,2048]{2,1,0:T(8,128)(2,1)} %param.29, f32[1024,512]{1,0:T(8,128)} %copy.103, f32[1024,512]{1,0:T(8,128)} %reshape.313, f32[1024,512]{1,0:T(8,128)} %divide_multiply_fusion, f32[512]{0:T(512)S(1)} %bitcast.256, f32[512]{0:T(512)S(1)} %mul.555, bf16[1024,1024]{1,0:T(8,128)(2,1)} %copy-done.17), kind=kOutput, calls=%fused_computation.31 | convolution fusion | flops 2155347968 | bytes 13635584 | tf_op jit(solution)/shard_map/dot_general | solution.py:120
  490.9 41.0 %reduce-scatter.5.cloned.1.call-done = bf16[1024,512]{1,0:T(8,128)(2,1)} async-done(((bf16[1024,2048]{1,0:T(8,128)(2,1)}), bf16[1024,512]{1,0:T(8,128)(2,1)}) %reduce-scatter.5.cloned.1.call-update) | async-done | bytes 1048592 | tf_op jit(solution)/shard_map/reduce_scatter | solution.py:128
  (286 shorter events, 205.4 us)
Async XLA Ops:
  6.5 39.6 %all-gather.8.cloned.1.call-start = ((), (), s32[]{:S(2)}) async-start(), calls=%async_computation.4 | async-start | bytes 5242880 | tf_op jit(solution)/shard_map/all_gather | solution.py:124
  7.3 177.6 %all-gather.10.cloned.1.call-start = ((), (), s32[]{:S(2)}) async-start(), calls=%async_computation.7 | async-start | bytes 1179648 | tf_op jit(solution)/shard_map/all_gather | solution.py:49
  15.3 6.1 %copy-start.23 = (f32[2,2048]{1,0:T(2,128)S(1)}, f32[2,2048]{1,0:T(2,128)}, u32[]{:S(2)}) copy-start(f32[2,2048]{1,0:T(2,128)} %param.19) | copy-start | bytes 49156
  84.6 16.2 %collective-permute-start = (bf16[3,512]{1,0:T(4,128)(2,1)}, bf16[3,512]{1,0:T(4,128)(2,1)}, u32[]{:S(2)}, u32[]{:S(2)}) collective-permute-start(bf16[3,512]{1,0:T(4,128)(2,1)} %slice.314), channel_id=1, source_target_pairs={{0,4},{4,8},{8,12},{12,16},{16,20},{20,24},{24,28},{1,5},{5,9},{9,... | collective-permute-start | bytes 9224 | tf_op jit(solution)/shard_map/ppermute | solution.py:18
  93.2 4.3 collective-permute-start.1
  117.0 20.4 %copy-start.33 = (f32[8]{0:T(128)S(1)}, f32[8]{0:T(128)}, u32[]{:S(2)}) copy-start(f32[8]{0:T(128)} %get-tuple-element.170) | copy-start | bytes 100
  117.0 20.6 %copy-start.43 = (u32[32]{0:T(128)S(1)}, u32[32]{0:T(128)}, u32[]{:S(2)}) copy-start(u32[32]{0:T(128)} %constant.98) | copy-start | bytes 388
  137.3 117.4 %reduce-scatter.3.cloned.1.call-start = ((), (), s32[]{:S(2)}) async-start(), calls=%async_computation.5 | async-start | bytes 5242880 | tf_op jit(solution)/shard_map/reduce_scatter | solution.py:128
  175.2 12.2 %copy-start.2 = (f32[64,8,8,128]{3,2,1,0:T(8,128)S(1)}, f32[64,8,8,128]{3,2,1,0:T(8,128)}, u32[]{:S(2)}) copy-start(f32[64,8,8,128]{3,2,1,0:T(8,128)} %copy-done.1) | copy-start | bytes 6291460
  218.8 35.9 %copy-start.11 = (bf16[1024,512]{1,0:T(8,128)(2,1)S(1)}, bf16[1024,512]{1,0:T(8,128)(2,1)}, u32[]{:S(2)}) copy-start(bf16[1024,512]{1,0:T(8,128)(2,1)} %param.17) | copy-start | bytes 3145732
  261.3 31.2 %all-to-all-start.1 = ((bf16[8,128,512]{2,1,0:T(8,128)(2,1)}), bf16[8,128,512]{2,1,0:T(8,128)(2,1)S(1)}, u32[]{:S(2)}, u32[]{:S(2)}) async-start(bf16[8,128,512]{2,1,0:T(8,128)(2,1)} %bitcast.42), calls=%async_computation.2 | async-start | bytes 2097152 | tf_op jit(solution)/shard_map/all_to_all | solution.py:143
  266.8 63.4 %all-gather.12.cloned.1.call-start = ((), (), s32[]{:S(2)}) async-start(), calls=%async_computation.8 | async-start | bytes 5242880 | tf_op jit(solution)/shard_map/all_gather | solution.py:124
  297.6 164.5 %all-gather.14.cloned.1.call-start = ((), (), s32[]{:S(2)}) async-start(), calls=%async_computation.9 | async-start | bytes 1179648 | tf_op jit(solution)/shard_map/all_gather | solution.py:49
  297.6 35.8 %copy-start.40 = (bf16[2,2048,256]{2,1,0:T(8,128)(2,1)S(1)}, bf16[2,2048,256]{2,1,0:T(8,128)(2,1)}, u32[]{:S(2)}) copy-start(bf16[2,2048,256]{2,1,0:T(8,128)(2,1)} %param.21) | copy-start | bytes 6291460
  303.1 30.3 %copy-start.25 = (f32[1,2048]{1,0:T(1,128)S(1)}, f32[1,2048]{1,0:T(1,128)}, u32[]{:S(2)}) copy-start(f32[1,2048]{1,0:T(1,128)} %get-tuple-element.155) | copy-start | bytes 24580
  333.6 6.3 %copy-start.39 = (f32[8]{0:T(128)S(1)}, f32[8]{0:T(128)}, u32[]{:S(2)}) copy-start(f32[8]{0:T(128)} %get-tuple-element.174) | copy-start | bytes 100
  333.6 6.3 %copy-start.42 = (bf16[2,2048,8]{1,2,0:T(8,128)(2,1)S(1)}, bf16[2,2048,8]{1,2,0:T(8,128)(2,1)}, u32[]{:S(2)}) copy-start(bf16[2,2048,8]{1,2,0:T(8,128)(2,1)} %param.22) | copy-start | bytes 196612
  335.0 6.3 %copy-start.20 = (bf16[1024,256]{1,0:T(8,128)(2,1)}, bf16[1024,256]{1,0:T(8,128)(2,1)S(1)}, u32[]{:S(2)}) copy-start(bf16[1024,256]{1,0:T(8,128)(2,1)S(1)} %convolution_convert_fusion.4) | copy-start | bytes 1572868
  335.6 43.2 %collective-permute-start.3 = (bf16[3,256]{1,0:T(4,128)(2,1)}, bf16[3,256]{1,0:T(4,128)(2,1)}, u32[]{:S(2)}, u32[]{:S(2)}) collective-permute-start(bf16[3,256]{1,0:T(4,128)(2,1)} %slice.336), channel_id=1, source_target_pairs={{0,4},{4,8},{8,12},{12,16},{16,20},{20,24},{24,28},{1,5},{5,9},{9,... | collective-permute-start | bytes 4616 | tf_op jit(solution)/shard_map/ppermute | solution.py:18
  376.0 6.2 %collective-permute-start.2 = (bf16[3,512]{1,0:T(4,128)(2,1)}, bf16[3,512]{1,0:T(4,128)(2,1)S(1)}, u32[]{:S(2)}, u32[]{:S(2)}) collective-permute-start(bf16[3,512]{1,0:T(4,128)(2,1)} %slice.330), channel_id=1, source_target_pairs={{0,4},{4,8},{8,12},{12,16},{16,20},{20,24},{24,28},{1,5},{5,9},{9,... | collective-permute-start | bytes 9224 | tf_op jit(solution)/shard_map/ppermute | solution.py:18
  397.7 20.5 %copy-start.32 = (f32[8]{0:T(128)S(1)}, f32[8]{0:T(128)}, u32[]{:S(2)}) copy-start(f32[8]{0:T(128)} %get-tuple-element.169) | copy-start | bytes 100
  418.2 113.7 %reduce-scatter.5.cloned.1.call-start = ((), (), s32[]{:S(2)}) async-start(), calls=%async_computation.6 | async-start | bytes 5242880 | tf_op jit(solution)/shard_map/reduce_scatter | solution.py:128
  452.5 12.1 %copy-start.4 = (f32[64,8,8,128]{3,2,1,0:T(8,128)S(1)}, f32[64,8,8,128]{3,2,1,0:T(8,128)}, u32[]{:S(2)}) copy-start(f32[64,8,8,128]{3,2,1,0:T(8,128)} %copy-done.3) | copy-start | bytes 6291460
  490.9 41.0 %copy-start = (bf16[1024,512]{1,0:T(8,128)(2,1)S(1)}, bf16[1024,512]{1,0:T(8,128)(2,1)}, u32[]{:S(2)}) copy-start(bf16[1024,512]{1,0:T(8,128)(2,1)} %gather_fusion.2) | copy-start | bytes 3145732
  (31 other events, 100.5 us)
Sparse Core Ops, SparseCore 0:
  8.9 37.1 all-gather.7
  137.5 41.2 all-gather.9
  213.8 40.8 reduce-scatter.2
  297.7 32.4 all-gather.11
  418.3 39.3 all-gather.13
  491.1 40.8 reduce-scatter.4
where the time goes:
time: 550 us; the launch traced here: 541 us
  waiting for transfers between devices  137 us (25%)
  other arithmetic  116 us (21%)
  local copies, waits for them, and re-layouts  110 us (20%)
  matrix products  94.1 us (17%)
  blocking collectives  48.4 us (9%)
  starting transfers between devices  20.4 us (4%)
  between operations  15.1 us (3%)
    reduce_scatter x2, waiting for transfers between devices, collect_heads(): lax.psum_scatter(partial_sum.astype(jnp.bfloat16), 'tp', scatter_dimensio...  63.5 us
    all_gather x2, waiting for transfers between devices, spread_features(): return lax.all_gather(piece, 'tp', axis=1, tiled=True)  51.1 us
    another operation x2, other arithmetic, mixer(): cumul = jnp.cumsum(log_blocks, axis=1)  46.6 us
    unnamed x2, blocking collectives  39.5 us
    all_to_all x1, waiting for transfers between devices, reorder_rows(): lax.all_to_all(payload, 'seq', split_axis=0, concat_axis=0, tiled=True)  21.2 us
    dot_general x2, matrix products, mixer(): jnp.einsum('chqk,ckhp->cqhp', intersection[:, None] * jnp.exp(spread), fe...  19.3 us
    reshape x4, local copies, waits for them, and re-layouts, mixer(): (inside + carried + correction).reshape(row_count, head_count, HEAD_DIM)  17.2 us
    unnamed x97, local copies, waits for them, and re-layouts  17.1 us
  transfers between devices with their start and end apart: 11, of which 6 were waited for; matrix products, arithmetic and copies ran while one was open for 24% of the time, Pallas kernels for 0%

commit v1 on v0

v1 whole, which is shorter than its diff:
```python
import functools

import jax
import jax.numpy as jnp
from jax import lax
from jax.experimental import pallas as pl
from jax.experimental.pallas import tpu as pltpu
from jax.sharding import PartitionSpec as P

HEAD_DIM = 64
STATE = 128
STRETCH = 128
LANES = 128
HALO = 16
ROWS = 256

highest = lax.Precision.HIGHEST
epsilon = 1e-05
f32 = jnp.float32
bf16 = jnp.bfloat16


def expander(inner):
    head = lax.broadcasted_iota(jnp.int32, (LANES, inner), 0)
    channel = lax.broadcasted_iota(jnp.int32, (LANES, inner), 1)
    return (head == channel // HEAD_DIM).astype(f32)


def expand(values, spreader):
    return jnp.dot(values, spreader, preferred_element_type=f32, precision=highest)


def scan_kernel(
    full_ref, halo_ref, gain_ref, w_ref, taps_ref, bias_ref, rate_ref, skip_ref,
    y_ref, z_ref, c_ref, cum_ref, end_ref, ext_ref, state_ref, sofar_ref,
):
    i = pl.program_id(0)
    rows = full_ref.shape[0]
    inner = y_ref.shape[1]
    mixed = inner + 2 * STATE
    heads = inner // HEAD_DIM
    spreader = expander(inner)

    def normed(v):
        wide = v.astype(f32)
        scale = lax.rsqrt(jnp.mean(wide * wide, axis=-1, keepdims=True) + epsilon)
        return (wide * scale * gain_ref[...]).astype(bf16)

    @pl.when(i == 0)
    def _():
        before = jnp.dot(normed(halo_ref[...]), w_ref[:, :mixed], preferred_element_type=f32)
        ext_ref[0:8, :] = before[HALO - 8 :, :].astype(bf16).astype(f32)
        state_ref[...] = jnp.zeros_like(state_ref)
        sofar_ref[...] = jnp.zeros_like(sofar_ref)

    projected = jnp.dot(normed(full_ref[...]), w_ref[...], preferred_element_type=f32)
    ext_ref[8 : 8 + rows, :] = projected[:, :mixed].astype(bf16).astype(f32)
    conv = jnp.zeros((rows, mixed), f32)
    count = taps_ref.shape[0]
    for k in range(count):
        conv = conv + taps_ref[k : k + 1, :] * ext_ref[9 - count + k : 9 - count + k + rows, :]
    conv = conv * jax.nn.sigmoid(conv)
    ext_ref[0:8, :] = ext_ref[rows : rows + 8, :]
    z_ref[...] = projected[:, mixed : mixed + inner].astype(bf16)
    raw = projected[:, mixed + inner :] + bias_ref[...]
    step = jnp.maximum(raw, 0.0) + jnp.log1p(jnp.exp(-jnp.abs(raw)))
    logs = -step * rate_ref[...]
    x = conv[:, :inner]
    b_all = conv[:, inner : inner + STATE]
    c_all = conv[:, inner + STATE :].astype(bf16)
    c_ref[...] = c_all
    feed = x * expand(step, spreader)

    row = lax.broadcasted_iota(jnp.int32, (STRETCH, STRETCH), 0)
    col = lax.broadcasted_iota(jnp.int32, (STRETCH, STRETCH), 1)
    lower = row >= col
    tri = lower.astype(f32)
    left = lax.broadcasted_iota(jnp.int32, (STRETCH, 2 * HEAD_DIM), 1) < HEAD_DIM
    state = state_ref[...]
    sofar = sofar_ref[...]
    for block in range(rows // STRETCH):
        part = slice(block * STRETCH, (block + 1) * STRETCH)
        cum = jnp.dot(tri, logs[part], preferred_element_type=f32, precision=highest)
        cum_t = cum.T
        last = cum[STRETCH - 1 : STRETCH, :]
        b_rows = b_all[part]
        c_rows = c_all[part]
        meet = lax.dot_general(
            c_rows, b_rows.astype(bf16), (((1,), (1,)), ((), ())), preferred_element_type=f32
        )
        factors = expand(
            jnp.concatenate([jnp.exp(cum), jnp.exp(last - cum)], axis=0), spreader
        )
        grown = factors[:STRETCH]
        feed_rows = feed[part]
        carried = jnp.dot(c_rows, state.astype(bf16), preferred_element_type=f32) * grown
        fresh = jnp.dot(
            b_rows.T.astype(bf16),
            (feed_rows * factors[STRETCH:]).astype(bf16),
            preferred_element_type=f32,
        )
        state = state * grown[STRETCH - 1 : STRETCH, :] + fresh
        carried = carried + skip_ref[...] * x[part]
        for pair in range(heads // 2):
            lanes = slice(pair * 2 * HEAD_DIM, (pair + 1) * 2 * HEAD_DIM)
            weights = []
            for h in (2 * pair, 2 * pair + 1):
                spread = jnp.where(lower, cum[:, h : h + 1] - cum_t[h : h + 1, :], -jnp.inf)
                weights.append((meet * jnp.exp(spread)).astype(bf16))
            fed = feed_rows[:, lanes]
            stacked = jnp.concatenate(
                [jnp.where(left, fed, 0.0), jnp.where(left, 0.0, fed)], axis=0
            ).astype(bf16)
            inside = jnp.dot(
                jnp.concatenate(weights, axis=1), stacked, preferred_element_type=f32
            )
            y_ref[part, lanes] = inside + carried[:, lanes]
        cum_ref[part, :] = cum + sofar[0:1, :]
        sofar = sofar + last
    state_ref[...] = state
    sofar_ref[...] = sofar

    @pl.when(i == pl.num_programs(0) - 1)
    def _():
        end_ref[0:STATE, :] = state.astype(bf16)
        total = expand(jnp.concatenate([sofar, sofar], axis=0), spreader)
        high = total.astype(bf16)
        rest = total - high.astype(f32)
        middle = rest.astype(bf16)
        low = (rest - middle.astype(f32)).astype(bf16)
        line = lax.broadcasted_iota(jnp.int32, total.shape, 0)
        end_ref[STATE:, :] = jnp.where(
            line == 0,
            high.astype(f32),
            jnp.where(line == 1, middle.astype(f32), low.astype(f32)),
        ).astype(bf16)


def out_kernel(
    y_ref, z_ref, c_ref, cum_ref, ends_ref, gain_ref, w_ref, o_ref, arriving_ref
):
    inner = y_ref.shape[1]
    own = lax.axis_index("seq")

    @pl.when(pl.program_id(0) == 0)
    def _():
        state = jnp.zeros((STATE, inner), f32)
        for m in range(ends_ref.shape[0]):
            tail = ends_ref[m, STATE:, :].astype(f32)
            log = tail[0:1] + tail[1:2] + tail[2:3]
            onward = state * jnp.exp(log) + ends_ref[m, :STATE, :].astype(f32)
            state = jnp.where(m < own, onward, state)
        arriving_ref[...] = state.astype(bf16)

    correction = jnp.dot(c_ref[...], arriving_ref[...], preferred_element_type=f32)
    correction = correction * expand(jnp.exp(cum_ref[...]), expander(inner))
    gate = z_ref[...].astype(f32)
    gated = (y_ref[...] + correction) * (gate * jax.nn.sigmoid(gate))
    pair = 2 * HEAD_DIM
    one = lax.broadcasted_iota(jnp.int32, (2 * pair, pair), 0) % pair // HEAD_DIM
    two = lax.broadcasted_iota(jnp.int32, (2 * pair, pair), 1) // HEAD_DIM
    averager = jnp.where(one == two, 1.0 / HEAD_DIM, 0.0).astype(bf16)
    square = gated * gated
    high = square.astype(bf16)
    low = (square - high.astype(f32)).astype(bf16)
    pieces = []
    for p in range(inner // pair):
        lanes = slice(p * pair, (p + 1) * pair)
        both = jnp.concatenate([high[:, lanes], low[:, lanes]], axis=1)
        mean = jnp.dot(both, averager, preferred_element_type=f32)
        pieces.append(
            (gated[:, lanes] * lax.rsqrt(mean + epsilon) * gain_ref[:, lanes]).astype(bf16)
        )
    mixed_heads = jnp.concatenate(pieces, axis=1)
    o_ref[...] = jnp.dot(mixed_heads, w_ref[...], preferred_element_type=f32).astype(bf16)


def whole(shape):
    return pl.BlockSpec(shape, lambda i: (0,) * len(shape))


def blocked(columns):
    return pl.BlockSpec((ROWS, columns), lambda i: (i, 0))


def mixer(full, halo, params):
    gain, weights, taps, bias, rate, skip, out_gain, w_out = params
    row_count, width = full.shape
    inner = w_out.shape[0]
    mixed = inner + 2 * STATE
    steps = row_count // ROWS
    limit = pltpu.CompilerParams(
        dimension_semantics=("arbitrary",), vmem_limit_bytes=48 * 1024 * 1024
    )
    y, z, c, cum, end = pl.pallas_call(
        scan_kernel,
        grid=(steps,),
        in_specs=[
            blocked(width), whole(halo.shape), whole(gain.shape), whole(weights.shape),
            whole(taps.shape), whole(bias.shape), whole(rate.shape), whole(skip.shape),
        ],
        out_specs=[
            blocked(inner), blocked(inner), blocked(STATE), blocked(LANES),
            whole((STATE + HALO, inner)),
        ],
        out_shape=[
            jax.ShapeDtypeStruct((row_count, inner), f32),
            jax.ShapeDtypeStruct((row_count, inner), bf16),
            jax.ShapeDtypeStruct((row_count, STATE), bf16),
            jax.ShapeDtypeStruct((row_count, LANES), f32),
            jax.ShapeDtypeStruct((STATE + HALO, inner), bf16),
        ],
        scratch_shapes=[
            pltpu.VMEM((ROWS + 8, mixed), f32),
            pltpu.VMEM((STATE, inner), f32),
            pltpu.VMEM((8, LANES), f32),
        ],
        compiler_params=limit,
        cost_estimate=pl.CostEstimate(
            flops=2 * row_count * width * weights.shape[1],
            bytes_accessed=2 * row_count * width + 2 * weights.size,
            transcendentals=0,
        ),
        name="scan_rows",
    )(full, halo, gain, weights, taps, bias, rate, skip)
    ends = lax.all_gather(end, "seq", axis=0)
    return pl.pallas_call(
        out_kernel,
        grid=(steps,),
        in_specs=[
            blocked(inner), blocked(inner), blocked(STATE), blocked(LANES),
            whole(ends.shape), whole(out_gain.shape), whole(w_out.shape),
        ],
        out_specs=blocked(w_out.shape[1]),
        out_shape=jax.ShapeDtypeStruct((row_count, w_out.shape[1]), bf16),
        scratch_shapes=[pltpu.VMEM((STATE, inner), bf16)],
        compiler_params=limit,
        cost_estimate=pl.CostEstimate(
            flops=2 * row_count * inner * w_out.shape[1],
            bytes_accessed=2 * row_count * w_out.shape[1] + 2 * w_out.size,
            transcendentals=0,
        ),
        name="project_out",
    )(y, z, c, cum, ends, out_gain, w_out)


def spread_features(piece):
    return lax.all_gather(piece, "tp", axis=1, tiled=True)


def halo_rows(piece):
    count = lax.axis_size("seq")
    tail = piece[piece.shape[0] - HALO :]
    return spread_features(lax.ppermute(tail, "seq", [(i, i + 1) for i in range(count - 1)]))


def collect_heads(partial_sum):
    return lax.psum_scatter(partial_sum, "tp", scatter_dimension=1, tiled=True).astype(f32)


def ranks(member):
    length = member.shape[-1]
    upto = jnp.arange(length)[:, None] <= jnp.arange(length)[None, :]
    counted = jnp.dot(member.astype(bf16), upto.astype(bf16), preferred_element_type=f32)
    return counted.astype(jnp.int32) - 1


def reorder_plans(col_order):
    count = lax.axis_size("seq")
    own = lax.axis_index("seq")
    length = col_order.shape[0]
    share = length // count
    orders = lax.all_gather(col_order, "seq", axis=0)
    mine = orders // length == own
    rank = ranks(mine)
    slot = jnp.where(mine, rank, -1)
    chosen = slot[:, None, :] == jnp.arange(share)[None, :, None]
    wanted = jnp.sum(jnp.where(chosen, (orders % length)[:, None, :], 0), axis=2).reshape(-1)
    hand = (wanted[:, None] == jnp.arange(length)[None, :]).astype(bf16)
    source = col_order // length
    from_each = source[None, :] == jnp.arange(count)[:, None]
    arrived = jnp.sum(
        jnp.where(from_each, ranks(from_each) + share * jnp.arange(count)[:, None], 0), axis=0
    )
    place = (arrived[:, None] == jnp.arange(length)[None, :]).astype(bf16)
    return hand, place


def pick(plan, rows):
    return jnp.dot(plan, rows, preferred_element_type=f32).astype(bf16)


def reorder_rows(stream, plans):
    hand, place = plans
    arrived = lax.all_to_all(pick(hand, stream), "seq", split_axis=0, concat_axis=0, tiled=True)
    return pick(place, arrived)


def body(
    tokens, col_order, in_gain, w_in, w_bc, w_dt, conv_x, conv_bc,
    dt_bias, a_log, d_skip, out_gain, w_out,
):
    inner = w_in.shape[3]
    pad = LANES - dt_bias.shape[1]

    def layer(which):
        weights = jnp.concatenate(
            [
                w_in[which, :, 0], w_bc[which], w_in[which, :, 1],
                jnp.pad(w_dt[which], ((0, 0), (0, pad))),
            ],
            axis=1,
        )
        return (
            in_gain[which][None],
            weights,
            jnp.concatenate([conv_x[which], conv_bc[which]], axis=1),
            jnp.pad(dt_bias[which], (0, pad))[None],
            jnp.pad(jnp.exp(a_log[which]), (0, pad))[None],
            jnp.repeat(d_skip[which], HEAD_DIM, total_repeat_length=inner)[None],
            out_gain[which][None],
            w_out[which],
        )

    plans = reorder_plans(col_order)
    first = mixer(spread_features(tokens), halo_rows(tokens), layer(0))
    row_result = (tokens.astype(f32) + collect_heads(first)).astype(bf16)
    own_rows = reorder_rows(row_result, plans)
    second = mixer(spread_features(own_rows), halo_rows(own_rows), layer(1))
    return (own_rows.astype(f32) + collect_heads(second)).astype(bf16)


def solution(mesh):
    placed = (
        P("seq", "tp"),
        P("seq"),
        P(),
        P(None, None, None, "tp"),
        P(),
        P(None, None, "tp"),
        P(None, None, "tp"),
        P(),
        P(None, "tp"),
        P(None, "tp"),
        P(None, "tp"),
        P(None, "tp"),
        P(None, "tp", None),
    )
    return jax.shard_map(
        body, mesh=mesh, in_specs=placed, out_specs=P("seq", "tp"), check_vma=False
    )
```

time: 550 us -> 382 us (0.69); the launches traced: 541 us -> 380 us
  other arithmetic: 116 us -> 19.8 us
  matrix products: 94.1 us -> 6.43 us
  Pallas kernels: 0 us -> 62.9 us
  local copies, waits for them, and re-layouts: 110 us -> 49.4 us
  waiting for transfers between devices: 137 us -> 172 us
  blocking collectives: 48.4 us -> 41.7 us
  starting transfers between devices: 20.4 us -> 13.9 us
    dot_general x20 -> x4, matrix products: 94.1 us -> 6.43 us  [the longest x2 5.78 us: pick(): return jnp.dot(plan, rows, preferred_element_type=f32).astype(bf16)]
    all_gather x2, waiting for transfers between devices: 0.01 us -> 77.2 us  [mixer(): ends = lax.all_gather(end, 'seq', axis=0)]
    pallas_call x0 -> x4, Pallas kernels: none -> 62.9 us  [the longest x2 45.4 us: mixer(): pl.pallas_call(scan_kernel, grid=(steps,), in_specs=[blocked(width), whol...]
    another operation x6 -> x1, other arithmetic: 46.7 us -> 0.01 us  [the longest x2 46.6 us: mixer(): cumul = jnp.cumsum(log_blocks, axis=1)]
    all_gather x0 -> x3, blocking collectives: none -> 41.7 us  [the longest x1 30.8 us: reorder_plans(): orders = lax.all_gather(col_order, 'seq', axis=0)]
    unnamed x2 -> x0, blocking collectives: 39.5 us -> none
    all_gather x2, waiting for transfers between devices: 51.1 us -> 13.6 us  [spread_features(): return lax.all_gather(piece, 'tp', axis=1, tiled=True)]
    reshape x12 -> x0, local copies, waits for them, and re-layouts: 31 us -> none  [the longest x4 17.2 us: mixer(): (inside + carried + correction).reshape(row_count, head_count, HEAD_DIM)]
  transfers between devices with their start and end apart: 11 -> 9, of which waited for: 6 -> 7; matrix products, arithmetic and copies ran while one was open for 24% -> 16% of each run, Pallas kernels for 0% -> 0%
where the time goes in v1:
time: 382 us; the launch traced here: 380 us
  waiting for transfers between devices  172 us (45%)
  Pallas kernels  62.9 us (16%)
  local copies, waits for them, and re-layouts  49.4 us (13%)
  blocking collectives  41.7 us (11%)
  other arithmetic  19.8 us (5%)
  starting transfers between devices  13.9 us (4%)
  between operations  13.7 us (4%)
  matrix products  6.43 us (2%)
    all_gather x2, waiting for transfers between devices, mixer(): ends = lax.all_gather(end, 'seq', axis=0)  77.2 us
    reduce_scatter x2, waiting for transfers between devices, collect_heads(): lax.psum_scatter(partial_sum, 'tp', scatter_dimension=1, tiled=True)  54.1 us
    pallas_call x2, Pallas kernels, mixer(): pl.pallas_call(scan_kernel, grid=(steps,), in_specs=[blocked(width), whol...  45.4 us
    all_gather x1, blocking collectives, reorder_plans(): orders = lax.all_gather(col_order, 'seq', axis=0)  30.8 us
    all_to_all x1, waiting for transfers between devices, reorder_rows(): lax.all_to_all(pick(hand, stream), 'seq', split_axis=0, concat_axis=0, ti...  25.3 us
    slice x1, local copies, waits for them, and re-layouts, layer(): w_in[which, :, 0]  17.8 us
    pallas_call x2, Pallas kernels, mixer(): pl.pallas_call(out_kernel, grid=(steps,), in_specs=[blocked(inner), block...  17.5 us
    all_gather x2, waiting for transfers between devices, spread_features(): return lax.all_gather(piece, 'tp', axis=1, tiled=True)  13.6 us
  transfers between devices with their start and end apart: 9, of which 7 were waited for; matrix products, arithmetic and copies ran while one was open for 16% of the time, Pallas kernels for 0%

profile of v1, /device:TPU:0, one launch (start us, length us, event | category | flops | bytes accessed | tf_op | source)
XLA Modules:
  0.0 380.3 jit_solution(10319278222639948302)
XLA Ops:
  8.0 4.9 %collective-permute-start = (bf16[16,512]{1,0:T(8,128)(2,1)S(1)}, bf16[16,512]{1,0:T(8,128)(2,1)S(1)}, u32[]{:S(2)}, u32[]{:S(2)}) collective-permute-start(bf16[16,512]{1,0:T(8,128)(2,1)S(1)} %slice.101), channel_id=1, source_target_pairs={{0,4},{4,8},{8,12},{12,16},{16,20},{20,24},{24,28},{1,5},{5,9},{9,... | collective-permute-start | bytes 49160 | tf_op jit(solution)/shard_map/ppermute | solution.py:254
  20.8 10.8 %select_select_fusion = (f32[512]{0:T(512)S(1)}, f32[512]{0:T(512)S(1)}) fusion(f32[]{:T(128)} %bitcast.44, f32[]{:T(128)} %bitcast.43, f32[]{:T(128)} %bitcast.42, f32[]{:T(128)} %bitcast.41, f32[]{:T(128)} %bitcast.40, f32[]{:T(128)} %bitcast.39, f32[]{:T(128)} %bitcast.38, f32[]{:T(128)} %bitcast.37, s32[4,128]{1,0:T(4,128)} %constant.138.clone.1, ...), kind=kLoop, calls=%fused_computation.68 | loop fusion | flops 15872 | bytes 6224 | tf_op jit(solution)/shard_map/jit(_take)/select_n | solution.py:320
  32.4 2.6 slice_bitcast_fusion.2
  35.1 17.8 %fusion.40 = (bf16[1,2048,1,512]{3,2,1,0:T(2,128)(2,1)}, bf16[1,2048,1,512]{3,2,1,0:T(2,128)(2,1)S(1)}, bf16[1,2048,1,512]{3,2,1,0:T(2,128)(2,1)S(1)}, bf16[1,2048,1,512]{3,2,1,0:T(2,128)(2,1)}) fusion(bf16[2,2048,2,512]{3,2,1,0:T(2,128)(2,1)} %param.22), kind=kLoop, calls=%fused_computation.95 | loop fusion | bytes 16777216 | tf_op jit(solution)/shard_map/slice | solution.py:309
  54.1 2.9 fusion.2.w_ref
  57.1 5.2 %all_gather.33.halo_ref = bf16[16,2048]{1,0:T(8,128)(2,1)S(1)} all-gather(bf16[16,512]{1,0:T(8,128)(2,1)S(1)} %collective-permute-done), channel_id=1, replica_groups=mesh['seq'=8,'tp'=4] {'tp'}, dimensions={1}, use_global_device_ids=true | all-gather | bytes 81920 | tf_op jit(solution)/shard_map/all_gather | solution.py:248
  62.3 22.7 %scan_rows.2 = (f32[1024,512]{1,0:T(8,128)S(1)}, bf16[1024,512]{1,0:T(8,128)(2,1)S(1)}, bf16[1024,128]{1,0:T(8,128)(2,1)S(1)}, f32[1024,128]{1,0:T(8,128)S(1)}, bf16[144,512]{1,0:T(8,128)(2,1)}) custom-call(bf16[1024,2048]{1,0:T(8,128)(2,1)} %all-gather.8.cloned.1.call-done.full_ref, bf16[16,2048]{1,0:T(8,128)(2,1)S(1)} %all_gather.33.halo_ref, ...), custom_call_target="tpu_custom_call" | custom-call | flops 5905580032 | bytes 9961472 | tf_op jit(solution)/shard_map/scan_rows/pallas_call | solution.py:195
  86.6 4.8 %slice_bitcast_fusion = (bf16[512,2048]{1,0:T(8,128)(2,1)}, bf16[512,2048]{1,0:T(8,128)(2,1)}) fusion(bf16[2,512,2048]{2,1,0:T(8,128)(2,1)} %param.31), kind=kLoop, calls=%fused_computation.19 | loop fusion | bytes 8388608 | tf_op jit(solution)/shard_map/squeeze | solution.py:322
  91.4 36.0 %all-gather.12.cloned.1.call-done = bf16[1152,512]{1,0:T(8,128)(2,1)} async-done(((bf16[144,512]{1,0:T(8,128)(2,1)}), bf16[1152,512]{1,0:T(8,128)(2,1)}) %all-gather.12.cloned.1.call-update) | async-done | bytes 1179664 | tf_op jit(solution)/shard_map/all_gather | solution.py:226
  129.7 8.8 %project_out.2 = bf16[1024,2048]{1,0:T(8,128)(2,1)} custom-call(f32[1024,512]{1,0:T(8,128)S(1)} %get-tuple-element.36.y_ref, bf16[1024,512]{1,0:T(8,128)(2,1)S(1)} %get-tuple-element.37.z_ref, bf16[1024,128]{1,0:T(8,128)(2,1)S(1)} %get-tuple-element.38.c_ref, f32[1024,128]{1,0:T(8,128)S(1)} %copy-done.3, bf16[8,144,512]{2,1,0:T(8,128)(2,1)S(1)} %bitcast.120, ...), custom_call_target="tpu_custom_call" | custom-call | flops 2147483648 | bytes 6291456 | tf_op jit(solution)/shard_map/project_out/pallas_call | solution.py:227
  139.2 30.8 %all-gather = s32[8192]{0:T(1024)S(1)} all-gather(s32[1024]{0:T(1024)S(1)} %copy-done.11), channel_id=2, replica_groups=mesh['seq'=8,'tp'=4] {'seq'}, dimensions={0}, use_global_device_ids=true | all-gather | bytes 36864 | tf_op jit(solution)/shard_map/all_gather | solution.py:273
  170.9 10.9 %reduce-scatter.3.cloned.1.call-done = bf16[1024,512]{1,0:T(8,128)(2,1)} async-done(((bf16[1024,2048]{1,0:T(8,128)(2,1)}), bf16[1024,512]{1,0:T(8,128)(2,1)}) %reduce-scatter.3.cloned.1.call-update) | async-done | bytes 1048592 | tf_op jit(solution)/shard_map/reduce_scatter | solution.py:258
  181.8 3.5 fusion.10
  185.3 5.5 %all-to-all-start = ((bf16[8,128,512]{2,1,0:T(8,128)(2,1)}), bf16[8,128,512]{2,1,0:T(8,128)(2,1)S(1)}, u32[]{:S(2)}, u32[]{:S(2)}) async-start(bf16[8,128,512]{2,1,0:T(8,128)(2,1)} %bitcast.24), calls=%async_computation.1 | async-start | bytes 2097152 | tf_op jit(solution)/shard_map/all_to_all | solution.py:295
  191.2 25.3 %all-to-all-done = bf16[8,128,512]{2,1,0:T(8,128)(2,1)S(1)} async-done(((bf16[8,128,512]{2,1,0:T(8,128)(2,1)}), bf16[8,128,512]{2,1,0:T(8,128)(2,1)S(1)}, u32[]{:S(2)}, u32[]{:S(2)}) %all-to-all-start) | async-done | bytes 1048608 | tf_op jit(solution)/shard_map/all_to_all | solution.py:295
  219.1 4.8 %copy_bitcast_fusion = (bf16[2048,512]{1,0:T(8,128)(2,1)S(1)}, bf16[2048,512]{1,0:T(8,128)(2,1)S(1)}) fusion(bf16[1,2048,1,512]{3,2,1,0:T(2,128)(2,1)} %get-tuple-element.49, bf16[1,2048,1,512]{3,2,1,0:T(2,128)(2,1)} %get-tuple-element.46), kind=kLoop, calls=%fused_computation.14 | loop fusion | bytes 8388608 | tf_op jit(solution)/shard_map/squeeze | solution.py:309
  223.9 3.0 fusion.3.w_ref
  227.6 3.3 collective-permute-start.1
  232.4 5.7 %all_gather.37.halo_ref = bf16[16,2048]{1,0:T(8,128)(2,1)S(1)} all-gather(bf16[16,512]{1,0:T(8,128)(2,1)S(1)} %collective-permute-done.1), channel_id=1, replica_groups=mesh['seq'=8,'tp'=4] {'tp'}, dimensions={1}, use_global_device_ids=true | all-gather | bytes 81920 | tf_op jit(solution)/shard_map/all_gather | solution.py:248
  238.1 13.6 %all-gather.10.cloned.1.call-done.full_ref = bf16[1024,2048]{1,0:T(8,128)(2,1)} async-done(((bf16[1024,512]{1,0:T(8,128)(2,1)}), bf16[1024,2048]{1,0:T(8,128)(2,1)}) %all-gather.10.cloned.1.call-update) | async-done | bytes 4194320 | tf_op jit(solution)/shard_map/all_gather | solution.py:248
  251.7 22.7 %scan_rows.3 = (f32[1024,512]{1,0:T(8,128)S(1)}, bf16[1024,512]{1,0:T(8,128)(2,1)S(1)}, bf16[1024,128]{1,0:T(8,128)(2,1)S(1)}, f32[1024,128]{1,0:T(8,128)S(1)}, bf16[144,512]{1,0:T(8,128)(2,1)}) custom-call(bf16[1024,2048]{1,0:T(8,128)(2,1)} %all-gather.10.cloned.1.call-done.full_ref, bf16[16,2048]{1,0:T(8,128)(2,1)S(1)} %all_gather.37.halo_ref, ...), custom_call_target="tpu_custom_call" | custom-call | flops 5905580032 | bytes 9961472 | tf_op jit(solution)/shard_map/scan_rows/pallas_call | solution.py:195
  275.3 41.2 %all-gather.14.cloned.1.call-done = bf16[1152,512]{1,0:T(8,128)(2,1)} async-done(((bf16[144,512]{1,0:T(8,128)(2,1)}), bf16[1152,512]{1,0:T(8,128)(2,1)}) %all-gather.14.cloned.1.call-update) | async-done | bytes 1179664 | tf_op jit(solution)/shard_map/all_gather | solution.py:226
  318.8 8.8 %project_out.3 = bf16[1024,2048]{1,0:T(8,128)(2,1)} custom-call(f32[1024,512]{1,0:T(8,128)S(1)} %get-tuple-element.41.y_ref, bf16[1024,512]{1,0:T(8,128)(2,1)S(1)} %get-tuple-element.42.z_ref, bf16[1024,128]{1,0:T(8,128)(2,1)S(1)} %get-tuple-element.43.c_ref, f32[1024,128]{1,0:T(8,128)S(1)} %copy-done.5, bf16[8,144,512]{2,1,0:T(8,128)(2,1)S(1)} %bitcast.121, ...), custom_call_target="tpu_custom_call" | custom-call | flops 2147483648 | bytes 6291456 | tf_op jit(solution)/shard_map/project_out/pallas_call | solution.py:227
  327.6 43.2 %reduce-scatter.5.cloned.1.call-done = bf16[1024,512]{1,0:T(8,128)(2,1)} async-done(((bf16[1024,2048]{1,0:T(8,128)(2,1)}), bf16[1024,512]{1,0:T(8,128)(2,1)}) %reduce-scatter.5.cloned.1.call-update) | async-done | bytes 1048592 | tf_op jit(solution)/shard_map/reduce_scatter | solution.py:258
  (71 shorter events, 27.8 us)
Async XLA Ops:
  6.5 55.7 %all-gather.8.cloned.1.call-start = ((), (), s32[]{:S(2)}) async-start(), calls=%async_computation.3 | async-start | bytes 5242880 | tf_op jit(solution)/shard_map/all_gather | solution.py:248
  7.3 120.1 %all-gather.12.cloned.1.call-start = ((), (), s32[]{:S(2)}) async-start(), calls=%async_computation.7 | async-start | bytes 1327104 | tf_op jit(solution)/shard_map/all_gather | solution.py:226
  8.0 49.0 %collective-permute-start = (bf16[16,512]{1,0:T(8,128)(2,1)S(1)}, bf16[16,512]{1,0:T(8,128)(2,1)S(1)}, u32[]{:S(2)}, u32[]{:S(2)}) collective-permute-start(bf16[16,512]{1,0:T(8,128)(2,1)S(1)} %slice.101), channel_id=1, source_target_pairs={{0,4},{4,8},{8,12},{12,16},{16,20},{20,24},{24,28},{1,5},{5,9},{9,... | collective-permute-start | bytes 49160 | tf_op jit(solution)/shard_map/ppermute | solution.py:254
  52.9 1.2 copy-start.8
  85.0 0.8 copy-start.2
  85.8 95.9 %reduce-scatter.3.cloned.1.call-start = ((), (), s32[]{:S(2)}) async-start(), calls=%async_computation.4 | async-start | bytes 5242880 | tf_op jit(solution)/shard_map/reduce_scatter | solution.py:258
  127.4 1.3 copy-start
  128.7 1.0 copy-start.3
  138.5 0.7 copy-start.11
  138.5 43.3 %copy-start.9 = (bf16[1024,512]{1,0:T(8,128)(2,1)S(1)}, bf16[1024,512]{1,0:T(8,128)(2,1)}, u32[]{:S(2)}) copy-start(bf16[1024,512]{1,0:T(8,128)(2,1)} %param.19) | copy-start | bytes 3145732
  185.3 31.2 %all-to-all-start = ((bf16[8,128,512]{2,1,0:T(8,128)(2,1)}), bf16[8,128,512]{2,1,0:T(8,128)(2,1)S(1)}, u32[]{:S(2)}, u32[]{:S(2)}) async-start(bf16[8,128,512]{2,1,0:T(8,128)(2,1)} %bitcast.24), calls=%async_computation.1 | async-start | bytes 2097152 | tf_op jit(solution)/shard_map/all_to_all | solution.py:295
  190.8 61.0 %all-gather.10.cloned.1.call-start = ((), (), s32[]{:S(2)}) async-start(), calls=%async_computation.5 | async-start | bytes 5242880 | tf_op jit(solution)/shard_map/all_gather | solution.py:248
  216.5 2.6 copy-start.10
  218.8 97.8 %all-gather.14.cloned.1.call-start = ((), (), s32[]{:S(2)}) async-start(), calls=%async_computation.8 | async-start | bytes 1327104 | tf_op jit(solution)/shard_map/all_gather | solution.py:226
  219.1 4.8 %copy-start.7 = (bf16[2048,256]{1,0:T(8,128)(2,1)S(1)}, bf16[2048,256]{1,0:T(8,128)(2,1)}, u32[]{:S(2)}) copy-start(bf16[2048,256]{1,0:T(8,128)(2,1)} %get-tuple-element.52) | copy-start | bytes 3145732
  223.9 7.1 %copy-start.12 = (f32[8]{0:T(128)S(1)}, f32[8]{0:T(128)}, u32[]{:S(2)}) copy-start(f32[8]{0:T(128)} %get-tuple-element.68) | copy-start | bytes 100
  223.9 7.1 %copy-start.13 = (f32[8]{0:T(128)S(1)}, f32[8]{0:T(128)}, u32[]{:S(2)}) copy-start(f32[8]{0:T(128)} %get-tuple-element.70) | copy-start | bytes 100
  227.6 4.8 %collective-permute-start.1 = (bf16[16,512]{1,0:T(8,128)(2,1)S(1)}, bf16[16,512]{1,0:T(8,128)(2,1)S(1)}, u32[]{:S(2)}, u32[]{:S(2)}) collective-permute-start(bf16[16,512]{1,0:T(8,128)(2,1)S(1)} %slice.161), channel_id=1, source_target_pairs={{0,4},{4,8},{8,12},{12,16},{16,20},{20,24},{24,28},{1,5},{5,9},{9,... | collective-permute-start | bytes 49160 | tf_op jit(solution)/shard_map/ppermute | solution.py:254
  274.4 0.8 copy-start.4
  275.2 95.6 %reduce-scatter.5.cloned.1.call-start = ((), (), s32[]{:S(2)}) async-start(), calls=%async_computation.6 | async-start | bytes 5242880 | tf_op jit(solution)/shard_map/reduce_scatter | solution.py:258
  316.5 1.3 copy-start.1
  317.8 1.0 copy-start.5
  327.6 43.3 %copy-start.6 = (bf16[1024,512]{1,0:T(8,128)(2,1)S(1)}, bf16[1024,512]{1,0:T(8,128)(2,1)}, u32[]{:S(2)}) copy-start(bf16[1024,512]{1,0:T(8,128)(2,1)} %fusion.11) | copy-start | bytes 3145732
Sparse Core Ops, SparseCore 0:
  8.9 37.1 all-gather.7
  85.9 41.4 all-gather.11
  138.6 43.0 reduce-scatter.2
  218.9 32.8 all-gather.9
  275.4 41.1 all-gather.13
  327.8 43.0 reduce-scatter.4

commit v2 on v1

--- a/solution.py
+++ b/solution.py
@@ -123,35 +123,11 @@
     @pl.when(i == pl.num_programs(0) - 1)
     def _():
         end_ref[0:STATE, :] = state.astype(bf16)
-        total = expand(jnp.concatenate([sofar, sofar], axis=0), spreader)
-        high = total.astype(bf16)
-        rest = total - high.astype(f32)
-        middle = rest.astype(bf16)
-        low = (rest - middle.astype(f32)).astype(bf16)
-        line = lax.broadcasted_iota(jnp.int32, total.shape, 0)
-        end_ref[STATE:, :] = jnp.where(
-            line == 0,
-            high.astype(f32),
-            jnp.where(line == 1, middle.astype(f32), low.astype(f32)),
-        ).astype(bf16)
-
-
-def out_kernel(
-    y_ref, z_ref, c_ref, cum_ref, ends_ref, gain_ref, w_ref, o_ref, arriving_ref
-):
+        end_ref[STATE:, :] = log_rows(expand(sofar, spreader)[0:1])
+
+
+def out_kernel(y_ref, z_ref, c_ref, cum_ref, arriving_ref, gain_ref, w_ref, o_ref):
     inner = y_ref.shape[1]
-    own = lax.axis_index("seq")
-
-    @pl.when(pl.program_id(0) == 0)
-    def _():
-        state = jnp.zeros((STATE, inner), f32)
-        for m in range(ends_ref.shape[0]):
-            tail = ends_ref[m, STATE:, :].astype(f32)
-            log = tail[0:1] + tail[1:2] + tail[2:3]
-            onward = state * jnp.exp(log) + ends_ref[m, :STATE, :].astype(f32)
-            state = jnp.where(m < own, onward, state)
-        arriving_ref[...] = state.astype(bf16)
-
     correction = jnp.dot(c_ref[...], arriving_ref[...], preferred_element_type=f32)
     correction = correction * expand(jnp.exp(cum_ref[...]), expander(inner))
     gate = z_ref[...].astype(f32)
@@ -175,6 +151,187 @@
     o_ref[...] = jnp.dot(mixed_heads, w_ref[...], preferred_element_type=f32).astype(bf16)
 
 
+def meet_all(partners):
+    barrier = pltpu.get_barrier_semaphore()
+    for partner in partners:
+        pl.semaphore_signal(
+            barrier, inc=1, device_id=partner, device_id_type=pl.DeviceIdType.MESH
+        )
+    pl.semaphore_wait(barrier, len(partners))
+
+
+def log_of(tail):
+    wide = tail.astype(f32)
+    return wide[0:1] + wide[1:2] + wide[2:3]
+
+
+def log_rows(log):
+    total = jnp.broadcast_to(log, (HALO, log.shape[1]))
+    high = total.astype(bf16).astype(f32)
+    middle = (total - high).astype(bf16).astype(f32)
+    low = (total - high) - middle
+    line = lax.broadcasted_iota(jnp.int32, total.shape, 0)
+    return jnp.where(line == 0, high, jnp.where(line == 1, middle, low)).astype(bf16)
+
+
+def exchange_kernel(
+    count, end_ref, arriving_ref, send_ref, got_ref, total_ref, prefix_ref, send_sem, recv_sem
+):
+    own = lax.axis_index("seq")
+    other = lax.axis_index("tp")
+    partners, uppers = [], []
+    size = 2
+    while size <= count:
+        place = own % size
+        base = own - place
+        partner = base + (1 - place if size == 2 else size - 2 - place + 2 * (place % 2))
+        partners.append((partner, other))
+        uppers.append(place // (size // 2) == 1)
+        size *= 2
+    meet_all(partners)
+    total_ref[...] = end_ref[:STATE, :].astype(f32)
+    prefix_ref[...] = jnp.zeros_like(prefix_ref)
+    total_log = log_of(end_ref[STATE:, :])
+    prefix_log = jnp.zeros_like(total_log)
+    for step, (partner, upper) in enumerate(zip(partners, uppers)):
+        if step:
+            send_ref[step - 1, :STATE, :] = total_ref[...].astype(bf16)
+            send_ref[step - 1, STATE:, :] = log_rows(total_log)
+        copy = pltpu.make_async_remote_copy(
+            src_ref=send_ref.at[step - 1] if step else end_ref,
+            dst_ref=got_ref.at[step],
+            send_sem=send_sem.at[step],
+            recv_sem=recv_sem.at[step],
+            device_id=partner,
+            device_id_type=pl.DeviceIdType.MESH,
+        )
+        copy.start()
+        copy.wait()
+        theirs = got_ref[step, :STATE, :].astype(f32)
+        their_log = log_of(got_ref[step, STATE:, :])
+        prefix = prefix_ref[...]
+        prefix_ref[...] = jnp.where(upper, theirs * jnp.exp(prefix_log) + prefix, prefix)
+        prefix_log = jnp.where(upper, prefix_log + their_log, prefix_log)
+        if step + 1 < len(partners):
+            mine = total_ref[...]
+            first = jnp.where(upper, theirs, mine)
+            then = jnp.where(upper, mine, theirs)
+            total_ref[...] = first * jnp.exp(jnp.where(upper, total_log, their_log)) + then
+            total_log = total_log + their_log
+    arriving_ref[...] = prefix_ref[...].astype(bf16)
+
+
+def exchange_states(end):
+    count = lax.axis_size("seq")
+    steps = count.bit_length() - 1
+    inner = end.shape[1]
+    vmem = pl.BlockSpec(memory_space=pltpu.VMEM)
+    return pl.pallas_call(
+        functools.partial(exchange_kernel, count),
+        in_specs=[vmem],
+        out_specs=vmem,
+        out_shape=jax.ShapeDtypeStruct((STATE, inner), bf16),
+        scratch_shapes=[
+            pltpu.VMEM((max(steps - 1, 1),) + end.shape, bf16),
+            pltpu.VMEM((steps,) + end.shape, bf16),
+            pltpu.VMEM((STATE, inner), f32),
+            pltpu.VMEM((STATE, inner), f32),
+            pltpu.SemaphoreType.DMA((steps,)),
+            pltpu.SemaphoreType.DMA((steps,)),
+        ],
+        compiler_params=pltpu.CompilerParams(collective_id=0, has_side_effects=True),
+        name="exchange_states",
+    )(end)
+
+
+def collect_kernel(
+    partial_ref, stream_ref, out_ref, near_ref, sum_ref, far_ref,
+    near_send, near_recv, far_send, far_recv,
+):
+    seq = lax.axis_index("seq")
+    own = lax.axis_index("tp")
+    chip, core = own // 2, own % 2
+    partner = (seq, chip * 2 + 1 - core)
+    across = (seq, (1 - chip) * 2 + core)
+    rows, width = out_ref.shape
+    chunks = near_send.shape[1]
+    size = rows // chunks
+
+    def columns(block):
+        return pl.ds(pl.multiple_of(block * width, LANES), width)
+
+    meet_all([partner, across])
+    near = []
+    for side, block in ((0, (1 - chip) * 2 + 1 - core), (1, chip * 2 + 1 - core)):
+        for k in range(chunks):
+            part = pl.ds(k * size, size)
+            copy = pltpu.make_async_remote_copy(
+                src_ref=partial_ref.at[part, columns(block)],
+                dst_ref=near_ref.at[side, part],
+                send_sem=near_send.at[side, k],
+                recv_sem=near_recv.at[side, k],
+                device_id=partner,
+                device_id_type=pl.DeviceIdType.MESH,
+            )
+            copy.start()
+            near.append(copy)
+    far = []
+    for k in range(chunks):
+        part = pl.ds(k * size, size)
+        near[k].wait_recv()
+        sum_ref[part, :] = (
+            partial_ref[part, columns((1 - chip) * 2 + core)].astype(f32)
+            + near_ref[0, part, :].astype(f32)
+        ).astype(bf16)
+        copy = pltpu.make_async_remote_copy(
+            src_ref=sum_ref.at[part],
+            dst_ref=far_ref.at[part],
+            send_sem=far_send.at[k],
+            recv_sem=far_recv.at[k],
+            device_id=across,
+            device_id_type=pl.DeviceIdType.MESH,
+        )
+        copy.start()
+        far.append(copy)
+    for k in range(chunks):
+        part = pl.ds(k * size, size)
+        near[chunks + k].wait_recv()
+        far[k].wait_recv()
+        out_ref[part, :] = (
+            stream_ref[part, :].astype(f32)
+            + partial_ref[part, columns(own)].astype(f32)
+            + near_ref[1, part, :].astype(f32)
+            + far_ref[part, :].astype(f32)
+        ).astype(bf16)
+    for copy in near + far:
+        copy.wait_send()
+
+
+def collect_heads(partial_sum, stream):
+    rows, width = stream.shape
+    chunks = 8
+    vmem = pl.BlockSpec(memory_space=pltpu.VMEM)
+    return pl.pallas_call(
+        collect_kernel,
+        in_specs=[vmem, vmem],
+        out_specs=vmem,
+        out_shape=jax.ShapeDtypeStruct(stream.shape, bf16),
+        scratch_shapes=[
+            pltpu.VMEM((2, rows, width), bf16),
+            pltpu.VMEM((rows, width), bf16),
+            pltpu.VMEM((rows, width), bf16),
+            pltpu.SemaphoreType.DMA((2, chunks)),
+            pltpu.SemaphoreType.DMA((2, chunks)),
+            pltpu.SemaphoreType.DMA((chunks,)),
+            pltpu.SemaphoreType.DMA((chunks,)),
+        ],
+        compiler_params=pltpu.CompilerParams(
+            collective_id=1, has_side_effects=True, vmem_limit_bytes=40 * 1024 * 1024
+        ),
+        name="collect_heads",
+    )(partial_sum, stream)
+
+
 def whole(shape):
     return pl.BlockSpec(shape, lambda i: (0,) * len(shape))
 
@@ -223,17 +380,16 @@
         ),
         name="scan_rows",
     )(full, halo, gain, weights, taps, bias, rate, skip)
-    ends = lax.all_gather(end, "seq", axis=0)
+    arriving = exchange_states(end)
     return pl.pallas_call(
         out_kernel,
         grid=(steps,),
         in_specs=[
             blocked(inner), blocked(inner), blocked(STATE), blocked(LANES),
-            whole(ends.shape), whole(out_gain.shape), whole(w_out.shape),
+            whole(arriving.shape), whole(out_gain.shape), whole(w_out.shape),
         ],
         out_specs=blocked(w_out.shape[1]),
         out_shape=jax.ShapeDtypeStruct((row_count, w_out.shape[1]), bf16),
-        scratch_shapes=[pltpu.VMEM((STATE, inner), bf16)],
         compiler_params=limit,
         cost_estimate=pl.CostEstimate(
             flops=2 * row_count * inner * w_out.shape[1],
@@ -241,7 +397,7 @@
             transcendentals=0,
         ),
         name="project_out",
-    )(y, z, c, cum, ends, out_gain, w_out)
+    )(y, z, c, cum, arriving, out_gain, w_out)
 
 
 def spread_features(piece):
@@ -254,36 +410,47 @@
     return spread_features(lax.ppermute(tail, "seq", [(i, i + 1) for i in range(count - 1)]))
 
 
-def collect_heads(partial_sum):
-    return lax.psum_scatter(partial_sum, "tp", scatter_dimension=1, tiled=True).astype(f32)
-
-
-def ranks(member):
-    length = member.shape[-1]
-    upto = jnp.arange(length)[:, None] <= jnp.arange(length)[None, :]
-    counted = jnp.dot(member.astype(bf16), upto.astype(bf16), preferred_element_type=f32)
-    return counted.astype(jnp.int32) - 1
+def plan_kernel(source_ref, local_ref, mine_ref, hand_ref, place_ref):
+    own = lax.axis_index("seq")
+    count, length = source_ref.shape
+    share = length // count
+    line = lax.broadcasted_iota(jnp.int32, (length, length), 0)
+    lane = lax.broadcasted_iota(jnp.int32, (length, length), 1)
+    upto = (line <= lane).astype(bf16)
+    device = lax.broadcasted_iota(jnp.int32, (count, length), 0)
+
+    def slots(member):
+        ones = jnp.where(member, 1.0, 0.0)
+        counted = jnp.dot(ones.astype(bf16), upto, preferred_element_type=f32)
+        return jnp.where(member, counted.astype(jnp.int32) - 1, -1)
+
+    slot = slots(source_ref[...] == own)
+    short = lax.broadcasted_iota(jnp.int32, (share, length), 0)
+    wide = lax.broadcasted_iota(jnp.int32, (share, length), 1)
+    for d in range(count):
+        chosen = slot[d : d + 1, :] == short
+        local = jnp.where(chosen, local_ref[d : d + 1, :], 0).astype(f32)
+        wanted = jnp.sum(local, axis=1, keepdims=True).astype(jnp.int32)
+        hand_ref[d * share : (d + 1) * share, :] = jnp.where(wanted == wide, 1.0, 0.0).astype(bf16)
+    from_each = mine_ref[...] == device
+    arrived = jnp.where(from_each, slots(from_each) + share * device, 0).astype(f32)
+    target = jnp.sum(arrived, axis=0, keepdims=True).astype(jnp.int32)
+    place_ref[...] = jnp.where(line == target, 1.0, 0.0).astype(bf16)
 
 
 def reorder_plans(col_order):
-    count = lax.axis_size("seq")
-    own = lax.axis_index("seq")
     length = col_order.shape[0]
-    share = length // count
     orders = lax.all_gather(col_order, "seq", axis=0)
-    mine = orders // length == own
-    rank = ranks(mine)
-    slot = jnp.where(mine, rank, -1)
-    chosen = slot[:, None, :] == jnp.arange(share)[None, :, None]
-    wanted = jnp.sum(jnp.where(chosen, (orders % length)[:, None, :], 0), axis=2).reshape(-1)
-    hand = (wanted[:, None] == jnp.arange(length)[None, :]).astype(bf16)
-    source = col_order // length
-    from_each = source[None, :] == jnp.arange(count)[:, None]
-    arrived = jnp.sum(
-        jnp.where(from_each, ranks(from_each) + share * jnp.arange(count)[:, None], 0), axis=0
-    )
-    place = (arrived[:, None] == jnp.arange(length)[None, :]).astype(bf16)
-    return hand, place
+    vmem = pl.BlockSpec(memory_space=pltpu.VMEM)
+    plan = jax.ShapeDtypeStruct((length, length), bf16)
+    return pl.pallas_call(
+        plan_kernel,
+        in_specs=[vmem] * 3,
+        out_specs=[vmem] * 2,
+        out_shape=[plan, plan],
+        compiler_params=pltpu.CompilerParams(vmem_limit_bytes=40 * 1024 * 1024),
+        name="reorder_plans",
+    )(orders // length, orders % length, (col_order // length)[None])
 
 
 def pick(plan, rows):
@@ -293,7 +460,9 @@
 def reorder_rows(stream, plans):
     hand, place = plans
     arrived = lax.all_to_all(pick(hand, stream), "seq", split_axis=0, concat_axis=0, tiled=True)
-    return pick(place, arrived)
+    return lax.dot_general(
+        place, arrived, (((0,), (0,)), ((), ())), preferred_element_type=f32
+    ).astype(bf16)
 
 
 def body(
@@ -323,11 +492,14 @@
         )
 
     plans = reorder_plans(col_order)
-    first = mixer(spread_features(tokens), halo_rows(tokens), layer(0))
-    row_result = (tokens.astype(f32) + collect_heads(first)).astype(bf16)
+    layers = [layer(0), layer(1)]
+    full = spread_features(tokens)
+    full, plans, layers = lax.optimization_barrier((full, plans, layers))
+    first = mixer(full, halo_rows(tokens), layers[0])
+    row_result = collect_heads(first, tokens)
     own_rows = reorder_rows(row_result, plans)
-    second = mixer(spread_features(own_rows), halo_rows(own_rows), layer(1))
-    return (own_rows.astype(f32) + collect_heads(second)).astype(bf16)
+    second = mixer(spread_features(own_rows), halo_rows(own_rows), layers[1])
+    return collect_heads(second, own_rows)
 
 
 def solution(mesh):

time: 382 us -> 346 us (0.906)
  waiting for transfers between devices: 172 us -> 24.5 us
  Pallas kernels: 62.9 us -> 149 us
  blocking collectives: 41.7 us -> 73.2 us
  local copies, waits for them, and re-layouts: 49.4 us -> 55.4 us
  starting transfers between devices: 13.9 us -> 8.28 us
    pallas_call x0 -> x5, Pallas kernels: none -> 91.8 us  [the longest x2 53.3 us: collect_heads(): pl.pallas_call(collect_kernel, in_specs=[vmem, vmem], out_specs=vmem, out...]
    all_gather x2 -> x0, waiting for transfers between devices: 77.2 us -> none  [mixer(): ends = lax.all_gather(end, 'seq', axis=0)]
    reduce_scatter x2 -> x0, waiting for transfers between devices: 54.1 us -> none  [collect_heads(): lax.psum_scatter(partial_sum, 'tp', scatter_dimension=1, tiled=True)]
    all_to_all x0 -> x1, blocking collectives: none -> 31.1 us  [reorder_rows(): lax.all_to_all(pick(hand, stream), 'seq', split_axis=0, concat_axis=0, ti...]
    all_to_all x1 -> x0, waiting for transfers between devices: 25.3 us -> none  [reorder_rows(): lax.all_to_all(pick(hand, stream), 'seq', split_axis=0, concat_axis=0, ti...]
    unnamed x30 -> x59, local copies, waits for them, and re-layouts: 8.19 us -> 24.4 us
    all_gather x2, waiting for transfers between devices: 13.6 us -> 22.4 us  [spread_features(): return lax.all_gather(piece, 'tp', axis=1, tiled=True)]
    all_to_all x1 -> x0, starting transfers between devices: 5.52 us -> none  [reorder_rows(): lax.all_to_all(pick(hand, stream), 'seq', split_axis=0, concat_axis=0, ti...]
  transfers between devices with their start and end apart: 9 -> 4, of which waited for: 7 -> 2; matrix products, arithmetic and copies ran while one was open for 16% -> 14% of each run, Pallas kernels for 0% -> 1%
where the time goes in v2:
time: 346 us; the launch traced here: 344 us
  Pallas kernels  149 us (43%)
  blocking collectives  73.2 us (21%)
  local copies, waits for them, and re-layouts  55.4 us (16%)
  waiting for transfers between devices  24.5 us (7%)
  other arithmetic  16.6 us (5%)
  between operations  13.7 us (4%)
  starting transfers between devices  8.28 us (2%)
  matrix products  3.53 us (1%)
    pallas_call x2, Pallas kernels, collect_heads(): pl.pallas_call(collect_kernel, in_specs=[vmem, vmem], out_specs=vmem, out...  53.3 us
    pallas_call x2, Pallas kernels, mixer(): pl.pallas_call(scan_kernel, grid=(steps,), in_specs=[blocked(width), whol...  44 us
    pallas_call x2, Pallas kernels, exchange_states(): pl.pallas_call(functools.partial(exchange_kernel, count), in_specs=[vmem]...  36.2 us
    all_to_all x1, blocking collectives, reorder_rows(): lax.all_to_all(pick(hand, stream), 'seq', split_axis=0, concat_axis=0, ti...  31.1 us
    all_gather x1, blocking collectives, reorder_plans(): orders = lax.all_gather(col_order, 'seq', axis=0)  31.1 us
    unnamed x59, local copies, waits for them, and re-layouts  24.4 us
    all_gather x2, waiting for transfers between devices, spread_features(): return lax.all_gather(piece, 'tp', axis=1, tiled=True)  22.4 us
    slice x1, local copies, waits for them, and re-layouts, layer(): w_in[which, :, 0]  16.7 us
  transfers between devices with their start and end apart: 4, of which 2 were waited for; matrix products, arithmetic and copies ran while one was open for 14% of the time, Pallas kernels for 1%

profile of v2, /device:TPU:0, one launch (start us, length us, event | category | flops | bytes accessed | tf_op | source)
XLA Modules:
  0.0 344.5 jit_solution(17170270589183289433)
XLA Ops:
  8.0 4.9 %collective-permute-start = (bf16[16,512]{1,0:T(8,128)(2,1)S(1)}, bf16[16,512]{1,0:T(8,128)(2,1)S(1)}, u32[]{:S(2)}, u32[]{:S(2)}) collective-permute-start(bf16[16,512]{1,0:T(8,128)(2,1)S(1)} %slice.125), channel_id=1, source_target_pairs={{0,4},{4,8},{8,12},{12,16},{16,20},{20,24},{24,28},{1,5},{5,9},{9,... | collective-permute-start | bytes 49160 | tf_op jit(solution)/shard_map/ppermute | solution.py:410
  12.9 31.1 %all-gather = s32[8192]{0:T(1024)S(1)} all-gather(s32[1024]{0:T(1024)} %param.20), channel_id=2, replica_groups=mesh['seq'=8,'tp'=4] {'seq'}, dimensions={0}, use_global_device_ids=true | all-gather | bytes 36864 | tf_op jit(solution)/shard_map/all_gather | solution.py:443
  51.3 4.2 %slice_bitcast_fusion = (bf16[512,2048]{1,0:T(8,128)(2,1)S(1)}, bf16[512,2048]{1,0:T(8,128)(2,1)}) fusion(bf16[2,512,2048]{2,1,0:T(8,128)(2,1)} %param.31), kind=kLoop, calls=%fused_computation.9 | loop fusion | bytes 8388608 | tf_op jit(solution)/shard_map/squeeze | solution.py:491
  56.2 10.1 %select_select_fusion = (f32[512]{0:T(512)S(1)}, f32[512]{0:T(512)S(1)}) fusion(f32[]{:T(128)} %bitcast.41, f32[]{:T(128)} %bitcast.40, f32[]{:T(128)} %bitcast.39, f32[]{:T(128)} %bitcast.38, f32[]{:T(128)} %bitcast.37, f32[]{:T(128)} %bitcast.36, f32[]{:T(128)} %bitcast.35, f32[]{:T(128)} %bitcast.34, s32[4,128]{1,0:T(4,128)S(1)} %copy-done.27, ...), kind=kLoop, calls=%fused_computation.37 | loop fusion | flops 15872 | bytes 6224 | tf_op jit(solution)/shard_map/jit(_take)/select_n | solution.py:489
  67.5 16.7 %fusion.8 = (bf16[1,2048,1,512]{3,2,1,0:T(2,128)(2,1)S(1)}, bf16[1,2048,1,512]{3,2,1,0:T(2,128)(2,1)S(1)}, bf16[1,2048,1,512]{3,2,1,0:T(2,128)(2,1)S(1)}, bf16[1,2048,1,512]{3,2,1,0:T(2,128)(2,1)S(1)}) fusion(bf16[2,2048,2,512]{3,2,1,0:T(2,128)(2,1)} %param.22), kind=kLoop, calls=%fused_computation.58 | loop fusion | bytes 16777216 | tf_op jit(solution)/shard_map/slice | solution.py:478
  86.7 2.9 fusion.3.w_ref
  89.7 2.9 fusion.2.w_ref
  92.5 2.3 reorder_plans.1
  97.5 5.4 %all_gather.21.halo_ref = bf16[16,2048]{1,0:T(8,128)(2,1)S(1)} all-gather(bf16[16,512]{1,0:T(8,128)(2,1)S(1)} %collective-permute-done), channel_id=1, replica_groups=mesh['seq'=8,'tp'=4] {'tp'}, dimensions={1}, use_global_device_ids=true | all-gather | bytes 81920 | tf_op jit(solution)/shard_map/all_gather | solution.py:404
  102.9 22.0 %scan_rows.2 = (f32[1024,512]{1,0:T(8,128)S(1)}, bf16[1024,512]{1,0:T(8,128)(2,1)S(1)}, bf16[1024,128]{1,0:T(8,128)(2,1)S(1)}, f32[1024,128]{1,0:T(8,128)S(1)}, bf16[144,512]{1,0:T(8,128)(2,1)S(1)}) custom-call(bf16[1024,2048]{1,0:T(8,128)(2,1)} %all-gather.4.cloned.1.call-done.full_ref, bf16[16,2048]{1,0:T(8,128)(2,1)S(1)} %all_gather.21.halo_ref, ...), custom_call_target="tpu_custom_call" | custom-call | flops 5905580032 | bytes 9961472 | tf_op jit(solution)/shard_map/scan_rows/pallas_call | solution.py:352
  127.7 17.2 %exchange_states.2.arriving_ref = bf16[128,512]{1,0:T(8,128)(2,1)} custom-call(bf16[144,512]{1,0:T(8,128)(2,1)} %copy-done.15), custom_call_target="tpu_custom_call" | custom-call | tf_op jit(solution)/shard_map/exchange_states/pallas_call | solution.py:229
  150.1 6.7 %project_out.2.partial_ref = bf16[1024,2048]{1,0:T(8,128)(2,1)} custom-call(f32[1024,512]{1,0:T(8,128)S(1)} %copy-done.6, bf16[1024,512]{1,0:T(8,128)(2,1)S(1)} %get-tuple-element.69.z_ref, bf16[1024,128]{1,0:T(8,128)(2,1)S(1)} %get-tuple-element.70.c_ref, f32[1024,128]{1,0:T(8,128)S(1)} %copy-done.12, bf16[128,512]{1,0:T(8,128)(2,1)S(1)} %copy-done.9, ...), custom_call_target="tpu_custom_call" | custom-call | flops 2147483648 | bytes 6291456 | tf_op jit(solution)/shard_map/project_out/pallas_call | solution.py:384
  156.8 2.2 copy-done.1
  159.0 27.3 %collect_heads.2 = bf16[1024,512]{1,0:T(8,128)(2,1)S(1)} custom-call(bf16[1024,2048]{1,0:T(8,128)(2,1)S(1)} %copy-done.1, bf16[1024,512]{1,0:T(8,128)(2,1)S(1)} %copy-done.3), custom_call_target="tpu_custom_call" | custom-call | tf_op jit(solution)/shard_map/collect_heads/pallas_call | solution.py:314
  187.5 31.1 %all_to_all.12 = bf16[8,128,512]{2,1,0:T(8,128)(2,1)S(1)} all-to-all(bf16[8,128,512]{2,1,0:T(8,128)(2,1)S(1)} %bitcast.126), channel_id=1, replica_groups=mesh['seq'=8,'tp'=4] {'seq'}, dimensions={0} | all-to-all | bytes 2097152 | tf_op jit(solution)/shard_map/all_to_all | solution.py:462
  218.7 2.3 convolution_convert_fusion.stream_ref
  221.7 3.3 collective-permute-start.1
  226.5 5.6 %all_gather.23.halo_ref = bf16[16,2048]{1,0:T(8,128)(2,1)S(1)} all-gather(bf16[16,512]{1,0:T(8,128)(2,1)S(1)} %collective-permute-done.1), channel_id=1, replica_groups=mesh['seq'=8,'tp'=4] {'tp'}, dimensions={1}, use_global_device_ids=true | all-gather | bytes 81920 | tf_op jit(solution)/shard_map/all_gather | solution.py:404
  232.0 22.4 %all-gather.6.cloned.1.call-done.full_ref = bf16[1024,2048]{1,0:T(8,128)(2,1)} async-done(((bf16[1024,512]{1,0:T(8,128)(2,1)}), bf16[1024,2048]{1,0:T(8,128)(2,1)}) %all-gather.6.cloned.1.call-update) | async-done | bytes 4194320 | tf_op jit(solution)/shard_map/all_gather | solution.py:404
  254.4 22.0 %scan_rows.3 = (f32[1024,512]{1,0:T(8,128)S(1)}, bf16[1024,512]{1,0:T(8,128)(2,1)S(1)}, bf16[1024,128]{1,0:T(8,128)(2,1)S(1)}, f32[1024,128]{1,0:T(8,128)S(1)}, bf16[144,512]{1,0:T(8,128)(2,1)S(1)}) custom-call(bf16[1024,2048]{1,0:T(8,128)(2,1)} %all-gather.6.cloned.1.call-done.full_ref, bf16[16,2048]{1,0:T(8,128)(2,1)S(1)} %all_gather.23.halo_ref, ...), custom_call_target="tpu_custom_call" | custom-call | flops 5905580032 | bytes 9961472 | tf_op jit(solution)/shard_map/scan_rows/pallas_call | solution.py:352
  279.2 19.0 %exchange_states.3.arriving_ref = bf16[128,512]{1,0:T(8,128)(2,1)} custom-call(bf16[144,512]{1,0:T(8,128)(2,1)} %copy-done.16), custom_call_target="tpu_custom_call" | custom-call | tf_op jit(solution)/shard_map/exchange_states/pallas_call | solution.py:229
  301.8 6.7 %project_out.3.partial_ref = bf16[1024,2048]{1,0:T(8,128)(2,1)} custom-call(f32[1024,512]{1,0:T(8,128)S(1)} %copy-done.8, bf16[1024,512]{1,0:T(8,128)(2,1)S(1)} %get-tuple-element.82.z_ref, bf16[1024,128]{1,0:T(8,128)(2,1)S(1)} %get-tuple-element.83.c_ref, f32[1024,128]{1,0:T(8,128)S(1)} %copy-done.14, bf16[128,512]{1,0:T(8,128)(2,1)S(1)} %copy-done.10, ...), custom_call_target="tpu_custom_call" | custom-call | flops 2147483648 | bytes 6291456 | tf_op jit(solution)/shard_map/project_out/pallas_call | solution.py:384
  308.5 2.2 copy-done
  310.7 26.0 %collect_heads.3 = bf16[1024,512]{1,0:T(8,128)(2,1)S(1)} custom-call(bf16[1024,2048]{1,0:T(8,128)(2,1)S(1)} %copy-done, bf16[1024,512]{1,0:T(8,128)(2,1)S(1)} %copy-done.4), custom_call_target="tpu_custom_call" | custom-call | tf_op jit(solution)/shard_map/collect_heads/pallas_call | solution.py:314
  (86 shorter events, 34.5 us)
Async XLA Ops:
  6.5 96.4 %all-gather.4.cloned.1.call-start = ((), (), s32[]{:S(2)}) async-start(), calls=%async_computation.1 | async-start | bytes 5242880 | tf_op jit(solution)/shard_map/all_gather | solution.py:404
  7.3 247.2 %all-gather.6.cloned.1.call-start = ((), (), s32[]{:S(2)}) async-start(), calls=%async_computation.2 | async-start | bytes 5242880 | tf_op jit(solution)/shard_map/all_gather | solution.py:404
  8.0 89.5 %collective-permute-start = (bf16[16,512]{1,0:T(8,128)(2,1)S(1)}, bf16[16,512]{1,0:T(8,128)(2,1)S(1)}, u32[]{:S(2)}, u32[]{:S(2)}) collective-permute-start(bf16[16,512]{1,0:T(8,128)(2,1)S(1)} %slice.125), channel_id=1, source_target_pairs={{0,4},{4,8},{8,12},{12,16},{16,20},{20,24},{24,28},{1,5},{5,9},{9,... | collective-permute-start | bytes 49160 | tf_op jit(solution)/shard_map/ppermute | solution.py:410
  51.3 4.2 %copy-start.25 = (f32[2,2048]{1,0:T(2,128)S(1)}, f32[2,2048]{1,0:T(2,128)}, u32[]{:S(2)}) copy-start(f32[2,2048]{1,0:T(2,128)} %param.21) | copy-start | bytes 49156
  51.3 4.2 %copy-start.26 = (f32[2,512]{1,0:T(2,128)S(1)}, f32[2,512]{1,0:T(2,128)}, u32[]{:S(2)}) copy-start(f32[2,512]{1,0:T(2,128)} %param.30) | copy-start | bytes 12292
  51.3 5.0 %copy-start.27 = (s32[4,128]{1,0:T(4,128)S(1)}, s32[4,128]{1,0:T(4,128)}, u32[]{:S(2)}) copy-start(s32[4,128]{1,0:T(4,128)} %constant.126.clone.1) | copy-start | bytes 6148
  51.3 15.1 %copy-start.24 = (bf16[2,2048,256]{2,1,0:T(8,128)(2,1)S(1)}, bf16[2,2048,256]{2,1,0:T(8,128)(2,1)}, u32[]{:S(2)}) copy-start(bf16[2,2048,256]{2,1,0:T(8,128)(2,1)} %param.23) | copy-start | bytes 6291460
  85.4 1.3 copy-start.21
  85.4 1.3 copy-start.23
  86.7 2.9 copy-start.22
  94.9 1.3 copy-start.17
  96.2 1.3 copy-start.19
  124.9 1.4 copy-start.5
  144.9 1.6 copy-start.2
  146.5 1.6 copy-start.6
  150.1 6.7 %copy-start.3 = (bf16[1024,512]{1,0:T(8,128)(2,1)S(1)}, bf16[1024,512]{1,0:T(8,128)(2,1)}, u32[]{:S(2)}) copy-start(bf16[1024,512]{1,0:T(8,128)(2,1)} %stream_ref.1) | copy-start | bytes 3145732
  156.8 2.2 copy-start.1
  159.0 27.3 %copy-start.20 = (bf16[1024,1024]{1,0:T(8,128)(2,1)S(1)}, bf16[1024,1024]{1,0:T(8,128)(2,1)}, u32[]{:S(2)}) copy-start(bf16[1024,1024]{1,0:T(8,128)(2,1)} %copy-done.19) | copy-start | bytes 6291460
  186.2 32.4 %copy-start.18 = (bf16[1024,1024]{1,0:T(8,128)(2,1)S(1)}, bf16[1024,1024]{1,0:T(8,128)(2,1)}, u32[]{:S(2)}) copy-start(bf16[1024,1024]{1,0:T(8,128)(2,1)} %copy-done.17) | copy-start | bytes 6291460
  221.7 4.8 %collective-permute-start.1 = (bf16[16,512]{1,0:T(8,128)(2,1)S(1)}, bf16[16,512]{1,0:T(8,128)(2,1)S(1)}, u32[]{:S(2)}, u32[]{:S(2)}) collective-permute-start(bf16[16,512]{1,0:T(8,128)(2,1)S(1)} %slice.161), channel_id=1, source_target_pairs={{0,4},{4,8},{8,12},{12,16},{16,20},{20,24},{24,28},{1,5},{5,9},{9,... | collective-permute-start | bytes 49160 | tf_op jit(solution)/shard_map/ppermute | solution.py:410
  276.4 1.3 copy-start.7
  298.2 1.6 copy-start.8
  301.8 6.7 %copy-start.4 = (bf16[1024,512]{1,0:T(8,128)(2,1)S(1)}, bf16[1024,512]{1,0:T(8,128)(2,1)}, u32[]{:S(2)}) copy-start(bf16[1024,512]{1,0:T(8,128)(2,1)} %convolution_convert_fusion.stream_ref) | copy-start | bytes 3145732
  308.5 2.2 copy-start
  (8 other events, 6.8 us)
Sparse Core Ops, SparseCore 0:
  8.9 37.1 all-gather.3
  221.1 33.2 all-gather.5

commit v3 on v2

--- a/solution.py
+++ b/solution.py
@@ -76,6 +76,7 @@
     lower = row >= col
     tri = lower.astype(f32)
     left = lax.broadcasted_iota(jnp.int32, (STRETCH, 2 * HEAD_DIM), 1) < HEAD_DIM
+    skip = expand(jnp.broadcast_to(skip_ref[...], (8, LANES)), spreader)[0:1]
     state = state_ref[...]
     sofar = sofar_ref[...]
     for block in range(rows // STRETCH):
@@ -100,7 +101,7 @@
             preferred_element_type=f32,
         )
         state = state * grown[STRETCH - 1 : STRETCH, :] + fresh
-        carried = carried + skip_ref[...] * x[part]
+        carried = carried + skip * x[part]
         for pair in range(heads // 2):
             lanes = slice(pair * 2 * HEAD_DIM, (pair + 1) * 2 * HEAD_DIM)
             weights = []
@@ -438,9 +439,8 @@
     place_ref[...] = jnp.where(line == target, 1.0, 0.0).astype(bf16)
 
 
-def reorder_plans(col_order):
+def reorder_plans(col_order, orders):
     length = col_order.shape[0]
-    orders = lax.all_gather(col_order, "seq", axis=0)
     vmem = pl.BlockSpec(memory_space=pltpu.VMEM)
     plan = jax.ShapeDtypeStruct((length, length), bf16)
     return pl.pallas_call(
@@ -469,7 +469,6 @@
     tokens, col_order, in_gain, w_in, w_bc, w_dt, conv_x, conv_bc,
     dt_bias, a_log, d_skip, out_gain, w_out,
 ):
-    inner = w_in.shape[3]
     pad = LANES - dt_bias.shape[1]
 
     def layer(which):
@@ -486,12 +485,14 @@
             jnp.concatenate([conv_x[which], conv_bc[which]], axis=1),
             jnp.pad(dt_bias[which], (0, pad))[None],
             jnp.pad(jnp.exp(a_log[which]), (0, pad))[None],
-            jnp.repeat(d_skip[which], HEAD_DIM, total_repeat_length=inner)[None],
+            jnp.pad(d_skip[which], (0, pad))[None],
             out_gain[which][None],
             w_out[which],
         )
 
-    plans = reorder_plans(col_order)
+    orders = lax.all_gather(col_order, "seq", axis=0)
+    tokens, orders = lax.optimization_barrier((tokens, orders))
+    plans = reorder_plans(col_order, orders)
     layers = [layer(0), layer(1)]
     full = spread_features(tokens)
     full, plans, layers = lax.optimization_barrier((full, plans, layers))

time: 346 us -> 332 us (0.960)
  other arithmetic: 16.6 us -> 6.5 us
  local copies, waits for them, and re-layouts: 55.4 us -> 50.2 us
    select_n x1 -> x0, other arithmetic: 10.1 us -> none  [layer(): jnp.repeat(d_skip[which], HEAD_DIM, total_repeat_length=inner)[None]]
    slice x1, local copies, waits for them, and re-layouts: 16.7 us -> 11.8 us  [layer(): w_in[which, :, 0]]
  transfers between devices with their start and end apart: 4 -> 4, of which waited for: 2 -> 2; matrix products, arithmetic and copies ran while one was open for 14% -> 10% of each run, Pallas kernels for 1% -> 1%
where the time goes in v3:
time: 332 us; the launch traced here: 331 us
  Pallas kernels  151 us (45%)
  blocking collectives  75.7 us (23%)
  local copies, waits for them, and re-layouts  50.2 us (15%)
  waiting for transfers between devices  23.9 us (7%)
  between operations  13.7 us (4%)
  starting transfers between devices  6.77 us (2%)
  other arithmetic  6.5 us (2%)
  matrix products  3.5 us (1%)
    pallas_call x2, Pallas kernels, collect_heads(): pl.pallas_call(collect_kernel, in_specs=[vmem, vmem], out_specs=vmem, out...  53.2 us
    pallas_call x2, Pallas kernels, mixer(): pl.pallas_call(scan_kernel, grid=(steps,), in_specs=[blocked(width), whol...  44.6 us
    pallas_call x2, Pallas kernels, exchange_states(): pl.pallas_call(functools.partial(exchange_kernel, count), in_specs=[vmem]...  36.9 us
    all_gather x1, blocking collectives, body(): orders = lax.all_gather(col_order, 'seq', axis=0)  32.5 us
    all_to_all x1, blocking collectives, reorder_rows(): lax.all_to_all(pick(hand, stream), 'seq', split_axis=0, concat_axis=0, ti...  32.2 us
    unnamed x59, local copies, waits for them, and re-layouts  24.5 us
    all_gather x2, waiting for transfers between devices, spread_features(): return lax.all_gather(piece, 'tp', axis=1, tiled=True)  22.4 us
    pallas_call x2, Pallas kernels, mixer(): pl.pallas_call(out_kernel, grid=(steps,), in_specs=[blocked(inner), block...  13.5 us
  transfers between devices with their start and end apart: 4, of which 2 were waited for; matrix products, arithmetic and copies ran while one was open for 10% of the time, Pallas kernels for 1%

profile of v3, /device:TPU:0, one launch (start us, length us, event | category | flops | bytes accessed | tf_op | source)
XLA Modules:
  0.0 330.8 jit_solution(148755525926330486)
XLA Ops:
  6.5 32.5 %all-gather = s32[8192]{0:T(1024)S(1)} all-gather(s32[1024]{0:T(1024)} %param.14), channel_id=2, replica_groups=mesh['seq'=8,'tp'=4] {'seq'}, dimensions={0}, use_global_device_ids=true | all-gather | bytes 36864 | tf_op jit(solution)/shard_map/all_gather | solution.py:493
  39.9 3.4 %collective-permute-start = (bf16[16,512]{1,0:T(8,128)(2,1)S(1)}, bf16[16,512]{1,0:T(8,128)(2,1)S(1)}, u32[]{:S(2)}, u32[]{:S(2)}) collective-permute-start(bf16[16,512]{1,0:T(8,128)(2,1)S(1)} %slice.102), channel_id=1, source_target_pairs={{0,4},{4,8},{8,12},{12,16},{16,20},{20,24},{24,28},{1,5},{5,9},{9,... | collective-permute-start | bytes 49160 | tf_op jit(solution)/shard_map/ppermute | solution.py:411
  50.8 4.1 %slice_bitcast_fusion = (bf16[512,2048]{1,0:T(8,128)(2,1)S(1)}, bf16[512,2048]{1,0:T(8,128)(2,1)}) fusion(bf16[2,512,2048]{2,1,0:T(8,128)(2,1)} %param.25), kind=kLoop, calls=%fused_computation.9 | loop fusion | bytes 8388608 | tf_op jit(solution)/shard_map/squeeze | solution.py:490
  56.2 11.8 %fusion.8 = (bf16[1,2048,1,512]{3,2,1,0:T(2,128)(2,1)S(1)}, bf16[1,2048,1,512]{3,2,1,0:T(2,128)(2,1)S(1)}, bf16[1,2048,1,512]{3,2,1,0:T(2,128)(2,1)S(1)}, bf16[1,2048,1,512]{3,2,1,0:T(2,128)(2,1)S(1)}) fusion(bf16[2,2048,2,512]{3,2,1,0:T(2,128)(2,1)S(1)} %copy-done.21), kind=kLoop, calls=%fused_computation.48 | loop fusion | bytes 16777216 | tf_op jit(solution)/shard_map/slice | solution.py:477
  70.6 2.9 fusion.3.w_ref
  73.6 2.9 fusion.2.w_ref
  76.4 2.3 reorder_plans.1
  81.4 5.4 %all_gather.21.halo_ref = bf16[16,2048]{1,0:T(8,128)(2,1)S(1)} all-gather(bf16[16,512]{1,0:T(8,128)(2,1)S(1)} %collective-permute-done), channel_id=1, replica_groups=mesh['seq'=8,'tp'=4] {'tp'}, dimensions={1}, use_global_device_ids=true | all-gather | bytes 81920 | tf_op jit(solution)/shard_map/all_gather | solution.py:405
  86.8 22.3 %scan_rows.2 = (f32[1024,512]{1,0:T(8,128)S(1)}, bf16[1024,512]{1,0:T(8,128)(2,1)S(1)}, bf16[1024,128]{1,0:T(8,128)(2,1)S(1)}, f32[1024,128]{1,0:T(8,128)S(1)}, bf16[144,512]{1,0:T(8,128)(2,1)S(1)}) custom-call(bf16[1024,2048]{1,0:T(8,128)(2,1)} %all-gather.4.cloned.1.call-done.full_ref, bf16[16,2048]{1,0:T(8,128)(2,1)S(1)} %all_gather.21.halo_ref, ...), custom_call_target="tpu_custom_call" | custom-call | flops 5905580032 | bytes 9961472 | tf_op jit(solution)/shard_map/scan_rows/pallas_call | solution.py:353
  112.0 17.9 %exchange_states.2.arriving_ref = bf16[128,512]{1,0:T(8,128)(2,1)} custom-call(bf16[144,512]{1,0:T(8,128)(2,1)} %copy-done.15), custom_call_target="tpu_custom_call" | custom-call | tf_op jit(solution)/shard_map/exchange_states/pallas_call | solution.py:230
  131.5 1.6 copy-done.6
  135.0 6.8 %project_out.2.partial_ref = bf16[1024,2048]{1,0:T(8,128)(2,1)} custom-call(f32[1024,512]{1,0:T(8,128)S(1)} %copy-done.6, bf16[1024,512]{1,0:T(8,128)(2,1)S(1)} %get-tuple-element.52.z_ref, bf16[1024,128]{1,0:T(8,128)(2,1)S(1)} %get-tuple-element.53.c_ref, f32[1024,128]{1,0:T(8,128)S(1)} %copy-done.12, bf16[128,512]{1,0:T(8,128)(2,1)S(1)} %copy-done.9, ...), custom_call_target="tpu_custom_call" | custom-call | flops 2147483648 | bytes 6291456 | tf_op jit(solution)/shard_map/project_out/pallas_call | solution.py:385
  141.8 2.2 copy-done.1
  144.0 27.3 %collect_heads.2 = bf16[1024,512]{1,0:T(8,128)(2,1)S(1)} custom-call(bf16[1024,2048]{1,0:T(8,128)(2,1)S(1)} %copy-done.1, bf16[1024,512]{1,0:T(8,128)(2,1)S(1)} %copy-done.3), custom_call_target="tpu_custom_call" | custom-call | tf_op jit(solution)/shard_map/collect_heads/pallas_call | solution.py:315
  172.5 32.2 %all_to_all.12 = bf16[8,128,512]{2,1,0:T(8,128)(2,1)S(1)} all-to-all(bf16[8,128,512]{2,1,0:T(8,128)(2,1)S(1)} %bitcast.60), channel_id=1, replica_groups=mesh['seq'=8,'tp'=4] {'seq'}, dimensions={0} | all-to-all | bytes 2097152 | tf_op jit(solution)/shard_map/all_to_all | solution.py:462
  204.7 2.3 convolution_convert_fusion.stream_ref
  207.7 3.3 %collective-permute-start.1 = (bf16[16,512]{1,0:T(8,128)(2,1)S(1)}, bf16[16,512]{1,0:T(8,128)(2,1)S(1)}, u32[]{:S(2)}, u32[]{:S(2)}) collective-permute-start(bf16[16,512]{1,0:T(8,128)(2,1)S(1)} %slice.104), channel_id=1, source_target_pairs={{0,4},{4,8},{8,12},{12,16},{16,20},{20,24},{24,28},{1,5},{5,9},{9,... | collective-permute-start | bytes 49160 | tf_op jit(solution)/shard_map/ppermute | solution.py:411
  212.4 5.6 %all_gather.23.halo_ref = bf16[16,2048]{1,0:T(8,128)(2,1)S(1)} all-gather(bf16[16,512]{1,0:T(8,128)(2,1)S(1)} %collective-permute-done.1), channel_id=1, replica_groups=mesh['seq'=8,'tp'=4] {'tp'}, dimensions={1}, use_global_device_ids=true | all-gather | bytes 81920 | tf_op jit(solution)/shard_map/all_gather | solution.py:405
  218.0 22.4 %all-gather.6.cloned.1.call-done.full_ref = bf16[1024,2048]{1,0:T(8,128)(2,1)} async-done(((bf16[1024,512]{1,0:T(8,128)(2,1)}), bf16[1024,2048]{1,0:T(8,128)(2,1)}) %all-gather.6.cloned.1.call-update) | async-done | bytes 4194320 | tf_op jit(solution)/shard_map/all_gather | solution.py:405
  240.4 22.2 %scan_rows.3 = (f32[1024,512]{1,0:T(8,128)S(1)}, bf16[1024,512]{1,0:T(8,128)(2,1)S(1)}, bf16[1024,128]{1,0:T(8,128)(2,1)S(1)}, f32[1024,128]{1,0:T(8,128)S(1)}, bf16[144,512]{1,0:T(8,128)(2,1)S(1)}) custom-call(bf16[1024,2048]{1,0:T(8,128)(2,1)} %all-gather.6.cloned.1.call-done.full_ref, bf16[16,2048]{1,0:T(8,128)(2,1)S(1)} %all_gather.23.halo_ref, ...), custom_call_target="tpu_custom_call" | custom-call | flops 5905580032 | bytes 9961472 | tf_op jit(solution)/shard_map/scan_rows/pallas_call | solution.py:353
  265.5 19.0 %exchange_states.3.arriving_ref = bf16[128,512]{1,0:T(8,128)(2,1)} custom-call(bf16[144,512]{1,0:T(8,128)(2,1)} %copy-done.16), custom_call_target="tpu_custom_call" | custom-call | tf_op jit(solution)/shard_map/exchange_states/pallas_call | solution.py:230
  288.1 6.7 %project_out.3.partial_ref = bf16[1024,2048]{1,0:T(8,128)(2,1)} custom-call(f32[1024,512]{1,0:T(8,128)S(1)} %copy-done.8, bf16[1024,512]{1,0:T(8,128)(2,1)S(1)} %get-tuple-element.65.z_ref, bf16[1024,128]{1,0:T(8,128)(2,1)S(1)} %get-tuple-element.66.c_ref, f32[1024,128]{1,0:T(8,128)S(1)} %copy-done.14, bf16[128,512]{1,0:T(8,128)(2,1)S(1)} %copy-done.10, ...), custom_call_target="tpu_custom_call" | custom-call | flops 2147483648 | bytes 6291456 | tf_op jit(solution)/shard_map/project_out/pallas_call | solution.py:385
  294.8 2.2 copy-done
  297.0 26.0 %collect_heads.3 = bf16[1024,512]{1,0:T(8,128)(2,1)S(1)} custom-call(bf16[1024,2048]{1,0:T(8,128)(2,1)S(1)} %copy-done, bf16[1024,512]{1,0:T(8,128)(2,1)S(1)} %copy-done.4), custom_call_target="tpu_custom_call" | custom-call | tf_op jit(solution)/shard_map/collect_heads/pallas_call | solution.py:315
  (84 shorter events, 31.8 us)
Async XLA Ops:
  6.5 80.3 %all-gather.4.cloned.1.call-start = ((), (), s32[]{:S(2)}) async-start(), calls=%async_computation.1 | async-start | bytes 5242880 | tf_op jit(solution)/shard_map/all_gather | solution.py:405
  39.1 201.3 %all-gather.6.cloned.1.call-start = ((), (), s32[]{:S(2)}) async-start(), calls=%async_computation.2 | async-start | bytes 5242880 | tf_op jit(solution)/shard_map/all_gather | solution.py:405
  39.9 41.5 %collective-permute-start = (bf16[16,512]{1,0:T(8,128)(2,1)S(1)}, bf16[16,512]{1,0:T(8,128)(2,1)S(1)}, u32[]{:S(2)}, u32[]{:S(2)}) collective-permute-start(bf16[16,512]{1,0:T(8,128)(2,1)S(1)} %slice.102), channel_id=1, source_target_pairs={{0,4},{4,8},{8,12},{12,16},{16,20},{20,24},{24,28},{1,5},{5,9},{9,... | collective-permute-start | bytes 49160 | tf_op jit(solution)/shard_map/ppermute | solution.py:411
  46.8 8.1 %copy-start.26 = (f32[2,2048]{1,0:T(2,128)S(1)}, f32[2,2048]{1,0:T(2,128)}, u32[]{:S(2)}) copy-start(f32[2,2048]{1,0:T(2,128)} %param.15) | copy-start | bytes 49156
  46.8 8.1 %copy-start.27 = (f32[2,512]{1,0:T(2,128)S(1)}, f32[2,512]{1,0:T(2,128)}, u32[]{:S(2)}) copy-start(f32[2,512]{1,0:T(2,128)} %param.24) | copy-start | bytes 12292
  46.8 8.2 %copy-start.25 = (bf16[2,2048,256]{2,1,0:T(8,128)(2,1)S(1)}, bf16[2,2048,256]{2,1,0:T(8,128)(2,1)}, u32[]{:S(2)}) copy-start(bf16[2,2048,256]{2,1,0:T(8,128)(2,1)} %param.17) | copy-start | bytes 6291460
  50.8 5.5 %copy-start.21 = (bf16[2,2048,2,512]{3,2,1,0:T(2,128)(2,1)S(1)}, bf16[2,2048,2,512]{3,2,1,0:T(2,128)(2,1)}, u32[]{:S(2)}) copy-start(bf16[2,2048,2,512]{3,2,1,0:T(2,128)(2,1)} %param.16) | copy-start | bytes 25165828
  69.3 1.3 copy-start.22
  69.3 1.3 copy-start.24
  70.6 2.9 copy-start.23
  78.8 1.3 copy-start.17
  80.1 1.3 copy-start.19
  109.2 1.4 copy-start.5
  129.9 1.6 copy-start.2
  131.5 1.6 copy-start.6
  135.0 6.8 %copy-start.3 = (bf16[1024,512]{1,0:T(8,128)(2,1)S(1)}, bf16[1024,512]{1,0:T(8,128)(2,1)}, u32[]{:S(2)}) copy-start(bf16[1024,512]{1,0:T(8,128)(2,1)} %stream_ref) | copy-start | bytes 3145732
  141.8 2.2 copy-start.1
  144.0 27.3 %copy-start.20 = (bf16[1024,1024]{1,0:T(8,128)(2,1)S(1)}, bf16[1024,1024]{1,0:T(8,128)(2,1)}, u32[]{:S(2)}) copy-start(bf16[1024,1024]{1,0:T(8,128)(2,1)} %copy-done.19) | copy-start | bytes 6291460
  171.2 33.5 %copy-start.18 = (bf16[1024,1024]{1,0:T(8,128)(2,1)S(1)}, bf16[1024,1024]{1,0:T(8,128)(2,1)}, u32[]{:S(2)}) copy-start(bf16[1024,1024]{1,0:T(8,128)(2,1)} %copy-done.17) | copy-start | bytes 6291460
  207.7 4.7 %collective-permute-start.1 = (bf16[16,512]{1,0:T(8,128)(2,1)S(1)}, bf16[16,512]{1,0:T(8,128)(2,1)S(1)}, u32[]{:S(2)}, u32[]{:S(2)}) collective-permute-start(bf16[16,512]{1,0:T(8,128)(2,1)S(1)} %slice.104), channel_id=1, source_target_pairs={{0,4},{4,8},{8,12},{12,16},{16,20},{20,24},{24,28},{1,5},{5,9},{9,... | collective-permute-start | bytes 49160 | tf_op jit(solution)/shard_map/ppermute | solution.py:411
  262.7 1.4 copy-start.7
  284.6 1.6 copy-start.8
  288.1 6.7 %copy-start.4 = (bf16[1024,512]{1,0:T(8,128)(2,1)S(1)}, bf16[1024,512]{1,0:T(8,128)(2,1)}, u32[]{:S(2)}) copy-start(bf16[1024,512]{1,0:T(8,128)(2,1)} %convolution_convert_fusion.stream_ref) | copy-start | bytes 3145732
  294.8 2.2 copy-start
  (8 other events, 6.8 us)
Sparse Core Ops, SparseCore 0:
  39.2 35.3 all-gather.3
  207.1 33.3 all-gather.5
